TPU v7x, 128 devices: a whole 4x4x4 slice. The times are simulated.
128 devices in a mesh: gx: 32 (over x, y, core), gy: 4 (over z).
Axes of the slice: x: 4, y: 4, z: 4, core: 2. Of those that a mesh axis runs over, the one named last changes fastest.
Arguments:
- layer_early: bfloat16 [4096, 8192], P(None, ('gx', 'gy')), may hold values from -48 to 48
- layer_late: bfloat16 [4096, 8192], P(('gx', 'gy')), may hold values from -48 to 48
Outputs:
- similarity: float32 [], replicated
- token_share: float32 [4096], P(('gx', 'gy'))
- early_rows: bfloat16 [4096, 8192], P(('gx', 'gy'))
- late_rows: bfloat16 [4096, 8192], P(('gx', 'gy'))
All inputs are finite; a program needn't handle non-finite values.
Results may differ from a plain program's by a relative error of at most 0.0015.
Values may be sent and summed in bfloat16 or wider, within the bound.
A program may use at most 128 MiB of HBM per device.

v0:
```python
import functools

import jax
import jax.numpy as jnp
from jax import lax
from jax.sharding import Mesh
from jax.sharding import PartitionSpec as P

GX_GY = ("gx_0", "gx_1", "gx_2", "gy")
GX = ("gx_0", "gx_1", "gx_2")


def one_axis_at_a_time(value, axes):
    return functools.reduce(lax.psum, axes, value)


def laid_out(tiles, dim):
    tiles = jnp.moveaxis(tiles, 0, dim)
    shape = tiles.shape
    return tiles.reshape(*shape[:dim], shape[dim] * shape[dim + 1], *shape[dim + 2 :])


def from_everyone(value, axis):
    copies = jnp.broadcast_to(value, (lax.axis_size(axis), *value.shape))
    return lax.all_to_all(copies, axis, split_axis=0, concat_axis=0, tiled=True)


def gathered_copies(value, axis, dim):
    return laid_out(from_everyone(value, axis), dim)


def in_one_piece(arrays, axis, dim, along):
    ends, at = ([], 0)
    for a in arrays[:-1]:
        at += a.shape[along]
        ends.append(at)
    both = jnp.concatenate(arrays, axis=along)
    return tuple(jnp.split(gathered_copies(both, axis, dim), ends, axis=along))


def in_one_piece_2(arrays, axis, dim, along):
    ends, at = ([], 0)
    for a in arrays[:-1]:
        at += a.shape[along]
        ends.append(at)
    both = jnp.concatenate(arrays, axis=along)
    return tuple(jnp.split(lax.all_gather(both, axis, axis=dim, tiled=True), ends, axis=along))


def split_up(value, dim, peers):
    shape = value.shape
    tiles = value.reshape(*shape[:dim], peers, shape[dim] // peers, *shape[dim + 1 :])
    return jnp.moveaxis(tiles, dim, 0)


def sent_and_summed(value, axis, dim):
    peers = lax.axis_size(axis)
    tiles = lax.all_to_all(split_up(value, dim, peers), axis, 0, 0, tiled=True)
    return jnp.sum(tiles, axis=0)


def pair_terms(left_early, left_late, right_early, right_late):
    dims = (((1,), (1,)), ((), ()))
    block_early = lax.dot_general(left_early, right_early, dims, preferred_element_type=jnp.float32)
    block_late = lax.dot_general(left_late, right_late, dims, preferred_element_type=jnp.float32)
    return (
        jnp.sum(block_early * block_late, axis=1),
        jnp.sum(block_early * block_early),
        jnp.sum(block_late * block_late),
    )


def body(layer_early, layer_late):
    total_rows = layer_early.shape[0]
    early_values = layer_early.astype(jnp.float32)
    early_cols = (early_values - jnp.mean(early_values, axis=0)).astype(jnp.bfloat16)
    late_values = layer_late.astype(jnp.float32)
    column_sums = one_axis_at_a_time(jnp.sum(late_values, axis=0), GX_GY)
    late_rows = (late_values - column_sums / total_rows).astype(jnp.bfloat16)
    early_rows = lax.all_to_all(early_cols, GX_GY, split_axis=0, concat_axis=1, tiled=True)
    block_early, block_late = in_one_piece((early_rows, late_rows), "gy", 0, 1)
    pieces = in_one_piece_2((early_rows, late_rows), GX, 0, 1)
    row_part, early_part, late_part = pair_terms(block_early, block_late, pieces[0], pieces[1])
    own_align = sent_and_summed(row_part, "gy", 0)
    total_kl, total_kk, total_ll = (
        one_axis_at_a_time(jnp.sum(row_part), GX_GY),
        one_axis_at_a_time(early_part, GX_GY),
        one_axis_at_a_time(late_part, GX_GY),
    )
    scale_norm = jnp.sqrt(total_kk * total_ll)
    similarity = total_kl / scale_norm
    token_share = total_rows * own_align / scale_norm
    return (similarity, token_share, early_rows, late_rows)


def solution(mesh):
    split = Mesh(mesh.devices.reshape(4, 4, 2, mesh.shape["gy"]), ("gx_0", "gx_1", "gx_2", "gy"))
    return jax.shard_map(
        body,
        mesh=split,
        in_specs=(P(None, GX_GY), P(GX_GY, None)),
        out_specs=(P(), P(GX_GY), P(GX_GY, None), P(GX_GY, None)),
        check_vma=False,
    )
```

profile of v0, /device:TPU:1, one launch (start us, length us, event | category | flops | bytes accessed | tf_op | source)
XLA Modules:
  0.0 263.7 jit_solution(14576012113702279938)
XLA Ops:
  7.2 0.0 copy-start
  7.2 1.3 convert_reduce_fusion.1
  8.5 1.2 fusion.6
  9.7 0.5 copy.9
  10.1 1.4 reshape.23
  11.5 11.5 %all-to-all-start = ((bf16[128,2,1024]{2,1,0:T(2,128)(2,1)}), bf16[128,2,1024]{2,1,0:T(2,128)(2,1)S(1)}, u32[]{:S(2)}, u32[]{:S(2)}) async-start(bf16[128,2,1024]{2,1,0:T(2,128)(2,1)} %reshape.23), calls=%async_computation | async-start | bytes 1048576 | tf_op jit(solution)/shard_map/all_to_all | solution.py:80
  23.0 0.0 all-gather.2.cloned.1.call-start
  23.1 0.0 copy-done
  23.1 0.1 convert_reduce_fusion
  23.2 15.1 %psum.112 = f32[8192]{0:T(1024)S(1)} all-reduce(f32[8192]{0:T(1024)S(1)} %convert_reduce_fusion), channel_id=1, replica_groups=mesh['gx_0'=4,'gx_1'=4,'gx_2'=2,'gy'=4] {'gx_0'}, use_global_device_ids=true, to_apply=%region_2.0 | all-reduce | flops 8192 | bytes 65536 | tf_op jit(solution)/shard_map/psum | solution.py:14
  38.3 13.2 %psum.113 = f32[8192]{0:T(1024)S(1)} all-reduce(f32[8192]{0:T(1024)S(1)} %psum.112), channel_id=1, replica_groups=mesh['gx_0'=4,'gx_1'=4,'gx_2'=2,'gy'=4] {'gx_1'}, use_global_device_ids=true, to_apply=%region_3.0 | all-reduce | flops 8192 | bytes 65536 | tf_op jit(solution)/shard_map/psum | solution.py:14
  51.6 10.1 %psum.114 = f32[8192]{0:T(1024)S(1)} all-reduce(f32[8192]{0:T(1024)S(1)} %psum.113), channel_id=1, replica_groups=mesh['gx_0'=4,'gx_1'=4,'gx_2'=2,'gy'=4] {'gx_2'}, use_global_device_ids=true, to_apply=%region_4.0 | all-reduce | flops 8192 | bytes 65536 | tf_op jit(solution)/shard_map/psum | solution.py:14
  61.6 14.0 %psum.115 = f32[8192]{0:T(1024)S(1)} all-reduce(f32[8192]{0:T(1024)S(1)} %psum.114), channel_id=1, replica_groups=mesh['gx_0'=4,'gx_1'=4,'gx_2'=2,'gy'=4] {'gy'}, use_global_device_ids=true, to_apply=%region_5.0 | all-reduce | flops 8192 | bytes 65536 | tf_op jit(solution)/shard_map/psum | solution.py:14
  75.7 0.1 fusion.7
  75.8 0.0 copy-start.2
  75.8 0.0 all-to-all-done
  75.8 0.6 reshape.24
  76.4 0.4 copy.10
  76.8 0.8 all_to_all.26
  77.7 0.0 copy-start.1
  77.7 1.1 pad_maximum_fusion
  78.8 0.0 all-gather.2.cloned.1.call-update
  78.8 0.0 copy-done.2
  78.8 1.6 broadcast_in_dim.2
  80.5 0.0 copy-done.1
  80.5 48.4 %all_to_all.33 = bf16[4,32,16384]{2,1,0:T(8,128)(2,1)} all-to-all(bf16[4,32,16384]{2,1,0:T(8,128)(2,1)S(1)} %broadcast_in_dim.2), channel_id=1, replica_groups=mesh['gx_0'=4,'gx_1'=4,'gx_2'=2,'gy'=4] {'gy'}, dimensions={0} | all-to-all | bytes 8388608 | tf_op jit(solution)/shard_map/all_to_all | solution.py:25
  128.9 63.8 %all-gather.2.cloned.1.call-done = bf16[1024,16384]{1,0:T(8,128)(2,1)} async-done(((bf16[32,16384]{1,0:T(8,128)(2,1)}), bf16[1024,16384]{1,0:T(8,128)(2,1)}) %all-gather.2.cloned.1.call-update) | async-done | bytes 33554448 | tf_op jit(solution)/shard_map/all_gather | solution.py:47
  192.6 9.9 %fusion = f32[128,1024]{1,0:T(8,128)S(1)} fusion(bf16[1024,16384]{1,0:T(8,128)(2,1)} %all-gather.2.cloned.1.call-done, bf16[128,16384]{1,0:T(8,128)(2,1)} %bitcast.5), kind=kOutput, calls=%fused_computation | convolution fusion | flops 2147483648 | bytes 19398656 | tf_op jit(solution)/shard_map/dot_general | solution.py:65
  202.5 12.8 %multiply_reduce_fusion.2 = (f32[128]{0:T(128)S(1)}, f32[]{:T(128)}, f32[]{:T(128)}, f32[]{:T(128)}) fusion(f32[128,1024]{1,0:T(8,128)S(1)} %fusion, bf16[1024,16384]{1,0:T(8,128)(2,1)} %all-gather.2.cloned.1.call-done, bf16[128,16384]{1,0:T(8,128)(2,1)} %bitcast.6), kind=kOutput, calls=%fused_computation.15 | convolution fusion | flops 2148401152 | bytes 19399180 | tf_op jit(solution)/shard_map/dot_general | solution.py:64
  215.3 0.7 all_to_all.28
  216.0 4.1 %all-to-all-start.2 = ((f32[4,1,32]{2,1,0:T(1,128)}), f32[4,1,32]{2,1,0:T(1,128)S(1)}, u32[]{:S(2)}, u32[]{:S(2)}) async-start(f32[4,1,32]{2,1,0:T(1,128)} %bitcast.3), calls=%async_computation.2 | async-start | bytes 4096 | tf_op jit(solution)/shard_map/all_to_all | solution.py:58
  220.1 9.2 %all-reduce.2 = (f32[]{:T(128)}, f32[]{:T(128)}, f32[]{:T(128)}) all-reduce(f32[]{:T(128)} %get-tuple-element.5, f32[]{:T(128)} %get-tuple-element.7, f32[]{:T(128)} %get-tuple-element.6), channel_id=1, replica_groups=mesh['gx_0'=4,'gx_1'=4,'gx_2'=2,'gy'=4] {'gx_0'}, use_global_device_ids=true, to_apply=%region_7.0 | all-reduce | flops 3 | bytes 24 | tf_op jit(solution)/shard_map/psum | solution.py:14
  229.3 7.2 %all-reduce.1 = (f32[]{:T(128)}, f32[]{:T(128)}, f32[]{:T(128)}) all-reduce(f32[]{:T(128)} %get-tuple-element.14, f32[]{:T(128)} %get-tuple-element.15, f32[]{:T(128)} %get-tuple-element.16), channel_id=1, replica_groups=mesh['gx_0'=4,'gx_1'=4,'gx_2'=2,'gy'=4] {'gx_1'}, use_global_device_ids=true, to_apply=%region_8.0 | all-reduce | flops 3 | bytes 24 | tf_op jit(solution)/shard_map/psum | solution.py:14
  236.5 7.1 %all-reduce.3 = (f32[]{:T(128)}, f32[]{:T(128)}, f32[]{:T(128)}) all-reduce(f32[]{:T(128)} %get-tuple-element.11, f32[]{:T(128)} %get-tuple-element.12, f32[]{:T(128)} %get-tuple-element.13), channel_id=1, replica_groups=mesh['gx_0'=4,'gx_1'=4,'gx_2'=2,'gy'=4] {'gx_2'}, use_global_device_ids=true, to_apply=%region_9.0 | all-reduce | flops 3 | bytes 24 | tf_op jit(solution)/shard_map/psum | solution.py:14
  243.7 9.6 %all-reduce = (f32[]{:T(128)}, f32[]{:T(128)}, f32[]{:T(128)}) all-reduce(f32[]{:T(128)} %get-tuple-element.17, f32[]{:T(128)} %get-tuple-element.18, f32[]{:T(128)} %get-tuple-element.19), channel_id=1, replica_groups=mesh['gx_0'=4,'gx_1'=4,'gx_2'=2,'gy'=4] {'gy'}, use_global_device_ids=true, to_apply=%region_10.0 | all-reduce | flops 3 | bytes 24 | tf_op jit(solution)/shard_map/psum | solution.py:14
  255.2 0.0 all-to-all-done.2
  255.2 0.5 multiply_divide_fusion
  (3 shorter events, 0.0 us)
Async XLA Ops:
  7.2 15.9 %copy-start = (bf16[32,8192]{1,0:T(8,128)(2,1)S(1)}, bf16[32,8192]{1,0:T(8,128)(2,1)}, u32[]{:S(2)}) copy-start(bf16[32,8192]{1,0:T(8,128)(2,1)} %param.3) | copy-start | bytes 1572868
  11.5 64.3 %all-to-all-start = ((bf16[128,2,1024]{2,1,0:T(2,128)(2,1)}), bf16[128,2,1024]{2,1,0:T(2,128)(2,1)S(1)}, u32[]{:S(2)}, u32[]{:S(2)}) async-start(bf16[128,2,1024]{2,1,0:T(2,128)(2,1)} %reshape.23), calls=%async_computation | async-start | bytes 1048576 | tf_op jit(solution)/shard_map/all_to_all | solution.py:80
  23.0 169.6 %all-gather.2.cloned.1.call-start = ((), (), s32[]{:S(2)}) async-start(), calls=%async_computation.3 | async-start | bytes 34603008 | tf_op jit(solution)/shard_map/all_gather | solution.py:47
  75.8 3.0 %copy-start.2 = (bf16[32,8192]{1,0:T(8,128)(2,1)}, bf16[32,8192]{1,0:T(8,128)(2,1)S(1)}, u32[]{:S(2)}) copy-start(bf16[32,8192]{1,0:T(8,128)(2,1)S(1)} %fusion.7) | copy-start | bytes 1572868
  77.7 2.8 %copy-start.1 = (bf16[32,8192]{1,0:T(8,128)(2,1)}, bf16[32,8192]{1,0:T(8,128)(2,1)S(1)}, u32[]{:S(2)}) copy-start(bf16[32,8192]{1,0:T(8,128)(2,1)S(1)} %all_to_all.26) | copy-start | bytes 1572868
  216.0 39.2 %all-to-all-start.2 = ((f32[4,1,32]{2,1,0:T(1,128)}), f32[4,1,32]{2,1,0:T(1,128)S(1)}, u32[]{:S(2)}, u32[]{:S(2)}) async-start(f32[4,1,32]{2,1,0:T(1,128)} %bitcast.3), calls=%async_computation.2 | async-start | bytes 4096 | tf_op jit(solution)/shard_map/all_to_all | solution.py:58
Sparse Core Ops, SparseCore 0:
  78.9 113.6 all-gather.1
where the time goes:
time: 265 us; the launch traced here: 264 us
  blocking collectives  134 us (51%)
  waiting for transfers between devices  63.8 us (24%)
  matrix products  22.7 us (9%)
  between operations  17.3 us (7%)
  starting transfers between devices  15.7 us (6%)
  local copies, waits for them, and re-layouts  6.01 us (2%)
  other arithmetic  4.35 us (2%)
    psum x8, blocking collectives, one_axis_at_a_time(): return functools.reduce(lax.psum, axes, value)  85.5 us
    all_gather x1, waiting for transfers between devices, in_one_piece_2(): lax.all_gather(both, axis, axis=dim, tiled=True)  63.8 us
    all_to_all x1, blocking collectives, from_everyone(): return lax.all_to_all(copies, axis, split_axis=0, concat_axis=0, tiled=True)  48.4 us
    dot_general x1, matrix products, pair_terms(): lax.dot_general(left_early, right_early, dims, preferred_element_type=jnp...  12.8 us
    all_to_all x1, starting transfers between devices, body(): lax.all_to_all(early_cols, GX_GY, split_axis=0, concat_axis=1, tiled=True)  11.5 us
    dot_general x1, matrix products, pair_terms(): lax.dot_general(left_late, right_late, dims, preferred_element_type=jnp.f...  9.86 us
  transfers between devices with their start and end apart: 3, of which 1 were waited for; matrix products, arithmetic and copies ran while one was open for 1% of the time, Pallas kernels for 0%

commit v1 on v0

v1 whole, which is shorter than its diff:
```python
import jax
import jax.numpy as jnp
from jax import lax
from jax.experimental import pallas as pl
from jax.experimental.pallas import tpu as pltpu
from jax.sharding import PartitionSpec as P

MESH = pl.DeviceIdType.MESH
F32 = jnp.float32
BF16 = jnp.bfloat16

SLOTS = ((0, 0), (1, 0), (0, 1), (1, 1), (1, 3), (3, 1))
TILES = (
    (0, 0, False),
    (1, 0, True),
    (2, 0, True),
    (1, 2, True),
    (4, 2, True),
    (5, 1, True),
    (4, 5, False),
    (3, 0, True),
    (3, 5, False),
    (4, 3, False),
)
K_CORE = 1
L_CORE = 0
PIECES = 8


def send(src, dst, send_sem, recv_sem, gx, gy):
    pltpu.make_async_remote_copy(
        src_ref=src,
        dst_ref=dst,
        send_sem=send_sem,
        recv_sem=recv_sem,
        device_id=(gx, gy),
        device_id_type=MESH,
    ).start()


def kernel(
    xt_hbm,
    late_hbm,
    share_ref,
    sim_ref,
    eout_hbm,
    lout_hbm,
    xt,
    late,
    cen,
    rt,
    blocks,
    gram,
    stage,
    parts,
    parts0,
    own_sum,
    plane_sums,
    mean_out,
    means,
    early_pieces,
    early_out,
    late_out,
    acc,
    row_cols,
    col_acc,
    msg,
    msg_in,
    total,
    total_in,
    load_sem,
    out_sem,
    late_send,
    late_recv,
    early_send,
    early_recv,
    pair_send,
    sums_send,
    sums_recv,
    mean_send,
    mean_recv,
    gather_send,
    gather_recv,
    rows_send,
    rows_recv,
    part_send,
    part_recv,
    part0_send,
    part0_recv,
    msg_send,
    msg_recv,
    total_send,
    total_recv,
):
    gx = lax.axis_index("gx")
    z = lax.axis_index("gy")
    core = lax.rem(gx, 2)
    chip = gx // 2
    x = chip // 4
    y = lax.rem(chip, 4)
    partner = gx + 1 - 2 * core
    k_dev = 2 * chip + K_CORE
    l_dev = 2 * chip + L_CORE
    is_k = core == K_CORE
    is_l = core == L_CORE

    def arrived(ref, sem):
        pltpu.make_async_remote_copy(
            src_ref=ref, dst_ref=ref, send_sem=sem, recv_sem=sem, device_id=(partner, z), device_id_type=MESH
        ).wait_recv()

    def left(ref, sem):
        pltpu.make_async_remote_copy(
            src_ref=ref, dst_ref=ref, send_sem=sem, recv_sem=sem, device_id=(partner, z), device_id_type=MESH
        ).wait_send()

    def chip_at(dx, dy):
        return lax.rem(x + dx, 4) * 4 + lax.rem(y + dy, 4)

    def level(dz):
        return lax.rem(z + dz, 4)

    barrier = pltpu.get_barrier_semaphore()

    @pl.loop(1, 16)
    def _(r):
        other = lax.rem(chip + r, 16)
        pl.semaphore_signal(barrier, inc=1, device_id=(2 * other, z), device_id_type=MESH)
        pl.semaphore_signal(barrier, inc=1, device_id=(2 * other + 1, z), device_id_type=MESH)

    for dz in (1, 2, 3):
        pl.semaphore_signal(barrier, inc=1, device_id=(2 * chip, level(dz)), device_id_type=MESH)
        pl.semaphore_signal(barrier, inc=1, device_id=(2 * chip + 1, level(dz)), device_id_type=MESH)
    pl.semaphore_signal(barrier, inc=1, device_id=(partner, z), device_id_type=MESH)

    load_x = pltpu.make_async_copy(xt_hbm, xt, load_sem.at[0])
    load_y = pltpu.make_async_copy(late_hbm, late, load_sem.at[1])
    load_x.start()
    load_y.start()
    load_x.wait()

    sums = jnp.zeros((64, 256), F32)
    for u in range(16):
        sums = sums + xt[:, 256 * u : 256 * (u + 1)].astype(F32)
    col_mean = jnp.sum(sums, axis=1, keepdims=True) / 4096.0
    for u in range(16):
        cen[u] = (xt[:, 256 * u : 256 * (u + 1)].astype(F32) - col_mean).astype(BF16)
    load_y.wait()

    pl.semaphore_wait(barrier, 37)

    my_rows = pl.ds(pl.multiple_of(32 * (4 * core + z), 32), 32)
    for dz in (1, 2, 3):
        to = level(dz)
        send(
            late.at[:, pl.ds(pl.multiple_of(2048 * to, 2048), 2048)],
            blocks.at[0, my_rows, :],
            late_send,
            late_recv,
            l_dev,
            to,
        )
    own_cols = pl.ds(pl.multiple_of(2048 * z, 2048), 2048)

    @pl.loop(1, 16)
    def _(r):
        other = lax.rem(chip + r, 16)
        send(cen.at[other], rt.at[gx], early_send, early_recv, 2 * other + K_CORE, z)

    @pl.when(is_k)
    def _():
        send(late.at[:, own_cols], blocks.at[0, my_rows, :], pair_send.at[0], late_recv, l_dev, z)
        rt[gx] = cen[chip]
        arrived(rt.at[0:31], early_recv)

        @pl.loop(0, 16)
        def _(u):
            cols = jnp.concatenate([rt[2 * u].astype(F32), rt[2 * u + 1].astype(F32)], axis=0)
            at = pl.ds(pl.multiple_of(128 * u, 128), 128)
            blocks[0, :, at] = cols.T.astype(BF16)

    @pl.when(is_l)
    def _():
        send(cen.at[chip], rt.at[gx], pair_send.at[0], early_recv, k_dev, z)
        blocks[0, my_rows, :] = late[:, own_cols]
        arrived(blocks.at[0, 0:224, :], late_recv)
        for c in range(4):
            at = slice(512 * c, 512 * (c + 1))
            part = jnp.zeros((32, 512), F32)
            for r in range(8):
                part = part + blocks[0, 32 * r : 32 * (r + 1), at].astype(F32)
            own_sum[:, at] = jnp.sum(part, axis=0, keepdims=True)
        plane_sums[chip] = own_sum[...]

        @pl.loop(1, 16)
        def _(r):
            other = lax.rem(chip + r, 16)
            send(own_sum, plane_sums.at[chip], sums_send, sums_recv, 2 * other + L_CORE, z)

        arrived(plane_sums.at[0:15], sums_recv)
        mean = plane_sums[0]
        for u in range(1, 16):
            mean = mean + plane_sums[u]
        mean_out[...] = mean / 4096.0
        means[z] = mean_out[...]
        for c in range(4):
            at = slice(512 * c, 512 * (c + 1))
            m = mean_out[:, at]
            for r in range(8):
                rows = slice(32 * r, 32 * (r + 1))
                blocks[0, rows, at] = (blocks[0, rows, at].astype(F32) - m).astype(BF16)

    def forward(src, dst, piece, ex, ey):
        rows = pl.ds(32 * piece, 32)
        to = 2 * chip_at(4 - ex, 4 - ey) + core
        send(blocks.at[src, rows, :], blocks.at[dst, rows, :], gather_send, gather_recv.at[dst - 1, piece], to, z)

    for i in range(PIECES):
        forward(0, 1, i, 1, 0)
        forward(0, 2, i, 0, 1)

    @pl.when(is_l)
    def _():
        send(mean_out, means.at[z], pair_send.at[1], mean_recv, k_dev, z)
        for dz in (1, 2, 3):
            send(mean_out, means.at[z], mean_send, mean_recv, k_dev, level(dz))
            send(mean_out, means.at[z], mean_send, mean_recv, l_dev, level(dz))

    @pl.when(is_k)
    def _():
        for dz in (1, 2, 3):
            for q in (0, 1):
                rows = pl.ds(pl.multiple_of(32 * (4 * q + level(dz)), 32), 32)
                send(blocks.at[0, rows, :], early_pieces.at[z], rows_send, rows_recv, 2 * chip + q, level(dz))
        rows = pl.ds(pl.multiple_of(32 * (4 * L_CORE + z), 32), 32)
        send(blocks.at[0, rows, :], early_pieces.at[z], pair_send.at[1], rows_recv, l_dev, z)
        early_pieces[z] = blocks[0, my_rows, :]

    dims = (((1,), (1,)), ((), ()))

    def product(t):
        a, b, _ = TILES[t]
        gram[t] = lax.dot_general(blocks[a], blocks[b], dims, preferred_element_type=F32)
        if t > 0:
            stage[t - 1] = gram[t].astype(BF16)
        for dz in (1, 2, 3):
            to = level(dz)
            rows = pl.ds(pl.multiple_of(64 * to, 64), 64)
            slot = dz - 1 + 4 * (1 - core)
            if t == 0:
                send(gram.at[0, rows, :], parts0.at[slot], part0_send, part0_recv, k_dev, to)
            else:
                send(stage.at[t - 1, rows, :], parts.at[t - 1, slot], part_send, part_recv.at[t - 1], k_dev, to)

        @pl.when(is_l)
        def _():
            rows = pl.ds(pl.multiple_of(64 * z, 64), 64)
            if t == 0:
                send(gram.at[0, rows, :], parts0.at[3], pair_send.at[2], part0_recv, k_dev, z)
            else:
                send(stage.at[t - 1, rows, :], parts.at[t - 1, 3], pair_send.at[3], part_recv.at[t - 1], k_dev, z)

    lane = lax.broadcasted_iota(jnp.int32, (64, 128), 1)

    def settle(t):
        _, b, both = TILES[t]
        rows = pl.ds(pl.multiple_of(64 * z, 64), 64)
        if t == 0:
            arrived(parts0, part0_recv)
            get = lambda s: parts0[s]
        else:
            arrived(parts.at[t - 1], part_recv.at[t - 1])
            get = lambda s: parts[t - 1, s].astype(F32)
        k = gram[t, rows, :] + ((get(0) + get(1)) + get(2))
        l = (get(3) + get(4)) + (get(5) + get(6))
        h = k * l
        row_cols[...] += jnp.where(lane == t, jnp.sum(h, axis=1, keepdims=True), 0.0)
        weight = 1.0
        if both:
            weight = 2.0
            col_acc[b : b + 1, :] += jnp.sum(h, axis=0, keepdims=True)
        acc[0] += weight * (k * k)
        acc[1] += weight * (l * l)
        acc[2] += weight * h

    product(0)

    @pl.when(is_k)
    def _():
        acc[...] = jnp.zeros_like(acc)
        row_cols[...] = jnp.zeros_like(row_cols)
        col_acc[...] = jnp.zeros_like(col_acc)

    for i in range(PIECES):
        rows = slice(32 * i, 32 * (i + 1))
        arrived(blocks.at[1, rows, :], gather_recv.at[0, i])
        forward(1, 4, i, 0, 3)
        arrived(blocks.at[2, rows, :], gather_recv.at[1, i])
        forward(2, 5, i, 3, 0)
        rows = pl.ds(32 * i, 32)
        to = 2 * chip_at(4 - (1 - core), 4 - core) + core
        send(blocks.at[2 - core, rows, :], blocks.at[3, rows, :], gather_send, gather_recv.at[2, i], to, z)

    for t in (1, 2, 3):
        product(t)

    @pl.when(is_k)
    def _():
        arrived(means, mean_recv)
        arrived(early_pieces.at[0:3], rows_recv)

    @pl.when(is_l)
    def _():
        arrived(means.at[0:3], mean_recv)
        arrived(early_pieces, rows_recv)

    for c in range(4):
        at = slice(2048 * c, 2048 * (c + 1))
        late_out[:, at] = (late[:, at].astype(F32) - means[c]).astype(BF16)
    low = lax.broadcasted_iota(jnp.int32, (32, 128), 1) < 64
    for u in range(16):
        p = [early_pieces[c, :, 128 * u : 128 * (u + 1)].astype(F32) for c in range(4)]
        turned = [pltpu.roll(v, 64, 1) for v in p]
        for j in range(2):
            first = jnp.where(low, p[2 * j], turned[2 * j + 1])
            second = jnp.where(low, turned[2 * j], p[2 * j + 1])
            early_out[:, 128 * (4 * u + j) : 128 * (4 * u + j + 1)] = first.astype(BF16)
            early_out[:, 128 * (4 * u + 2 + j) : 128 * (4 * u + 3 + j)] = second.astype(BF16)
    put_e = pltpu.make_async_copy(early_out, eout_hbm, out_sem.at[0])
    put_l = pltpu.make_async_copy(late_out, lout_hbm, out_sem.at[1])
    put_e.start()
    put_l.start()

    for i in range(PIECES):
        arrived(blocks.at[4, 32 * i : 32 * (i + 1), :], gather_recv.at[3, i])
    product(4)
    for i in range(PIECES):
        arrived(blocks.at[5, 32 * i : 32 * (i + 1), :], gather_recv.at[4, i])
    product(5)
    product(6)

    @pl.when(is_k)
    def _():
        for t in (0, 1, 2, 3):
            settle(t)

    for i in range(PIECES):
        arrived(blocks.at[3, 32 * i : 32 * (i + 1), :], gather_recv.at[2, i])
    for t in (7, 8, 9):
        product(t)

    @pl.when(is_k)
    def _():
        for t in (4, 5, 6, 7, 8, 9):
            settle(t)
        sides = row_cols[...]
        turned = jnp.concatenate([sides] * 4, axis=0).T
        mine = lax.broadcasted_iota(jnp.int32, (1, 256), 1) // 64 == z
        scal_lane = lax.broadcasted_iota(jnp.int32, (1, 128), 1)
        scal = jnp.zeros((1, 128), F32)
        for j in range(3):
            s = jnp.sum(jnp.sum(acc[j], axis=0, keepdims=True), axis=1, keepdims=True)
            scal = jnp.where(scal_lane == j, s, scal)
        for dx in range(4):
            for dy in range(4):
                r = 4 * dx + dy
                if (dx, dy) in SLOTS:
                    slot = SLOTS.index((dx, dy))
                    row = jnp.zeros((1, 256), F32)
                    for t, (a, _, _) in enumerate(TILES):
                        if a == slot:
                            row = row + turned[t : t + 1, :]
                    msg[r, :, 0:256] = col_acc[slot : slot + 1, :] + jnp.where(mine, row, 0.0)
                else:
                    msg[r, :, 0:256] = jnp.zeros((1, 256), F32)
                msg[r, :, 256:384] = scal
        for dx in range(4):
            for dy in range(4):
                r = 4 * dx + dy
                if r:
                    send(msg.at[r], msg_in.at[r], msg_send, msg_recv, 2 * chip_at(dx, dy) + K_CORE, z)
        msg_in[0] = msg[0]
        arrived(msg_in.at[0:15], msg_recv)
        s = msg_in[0]
        for r in range(1, 16):
            s = s + msg_in[r]
        total[...] = s
        for dz in (1, 2, 3):
            send(total, total_in.at[dz - 1], total_send, total_recv, k_dev, level(dz))
            send(total, total_in.at[dz - 1], total_send, total_recv, l_dev, level(dz))
        send(total, total_in.at[3], pair_send.at[2], total_recv, l_dev, z)
        total_in[3] = total[...]
        arrived(total_in.at[0:3], total_recv)

    @pl.when(is_l)
    def _():
        arrived(total_in, total_recv)

    final = (total_in[0] + total_in[1]) + (total_in[2] + total_in[3])
    scal_lane = lax.broadcasted_iota(jnp.int32, (1, 128), 1)
    scal = final[:, 256:384]
    kk, ll, kl = (jnp.sum(jnp.where(scal_lane == j, scal, 0.0), axis=1, keepdims=True) for j in range(3))
    norm = jnp.sqrt(kk * ll)
    sim_ref[...] = jnp.broadcast_to(kl / norm, (1, 128))
    half = jnp.where(core == 0, final[:, 0:128], final[:, 128:256])
    tokens = half
    for j in (1, 2, 3):
        tokens = jnp.where(z == j, pltpu.roll(half, 128 - 32 * j, 1), tokens)
    share_ref[...] = 4096.0 * tokens / norm

    put_e.wait()
    put_l.wait()
    left(late.at[:, 0:6144], late_send)
    left(cen.at[0:15], early_send)
    left(blocks.at[1:6], gather_send)
    left(parts.at[:, 0:3], part_send)
    left(parts0.at[0:3], part0_send)

    @pl.when(is_k)
    def _():
        left(late.at[:, 0:2048], pair_send.at[0])
        left(early_pieces.at[0], pair_send.at[1])
        left(total, pair_send.at[2])
        left(blocks.at[0, 0:192, :], rows_send)
        left(msg.at[0:15], msg_send)
        left(msg.at[0:6], total_send)

    @pl.when(is_l)
    def _():
        left(cen.at[0], pair_send.at[0])
        left(mean_out, pair_send.at[1])
        left(parts0.at[0], pair_send.at[2])
        left(parts.at[:, 0], pair_send.at[3])
        left(plane_sums.at[0:15], sums_send)
        left(plane_sums.at[0:6], mean_send)


def body(layer_early, layer_late):
    vm = pltpu.VMEM
    dma = pltpu.SemaphoreType.DMA
    hbm = pl.BlockSpec(memory_space=pltpu.HBM)
    whole = pl.BlockSpec(memory_space=pltpu.VMEM)
    share, sim, early_rows, late_rows = pl.pallas_call(
        kernel,
        out_shape=(
            jax.ShapeDtypeStruct((1, 128), F32),
            jax.ShapeDtypeStruct((1, 128), F32),
            jax.ShapeDtypeStruct((32, 8192), BF16),
            jax.ShapeDtypeStruct((32, 8192), BF16),
        ),
        in_specs=[hbm, hbm],
        out_specs=(whole, whole, hbm, hbm),
        scratch_shapes=[
            vm((64, 4096), BF16),
            vm((32, 8192), BF16),
            vm((16, 64, 256), BF16),
            vm((32, 64, 256), BF16),
            vm((6, 256, 2048), BF16),
            vm((10, 256, 256), F32),
            vm((9, 256, 256), BF16),
            vm((9, 7, 64, 256), BF16),
            vm((7, 64, 256), F32),
            vm((1, 2048), F32),
            vm((16, 1, 2048), F32),
            vm((1, 2048), F32),
            vm((4, 1, 2048), F32),
            vm((4, 32, 2048), BF16),
            vm((32, 8192), BF16),
            vm((32, 8192), BF16),
            vm((3, 64, 256), F32),
            vm((64, 128), F32),
            vm((8, 256), F32),
            vm((16, 1, 384), F32),
            vm((16, 1, 384), F32),
            vm((1, 384), F32),
            vm((4, 1, 384), F32),
            dma((2,)),
            dma((2,)),
            dma,
            dma,
            dma,
            dma,
            dma((4,)),
            dma,
            dma,
            dma,
            dma,
            dma,
            dma((5, PIECES)),
            dma,
            dma,
            dma,
            dma((9,)),
            dma,
            dma,
            dma,
            dma,
            dma,
            dma,
        ],
        compiler_params=pltpu.CompilerParams(collective_id=0, has_side_effects=True, vmem_limit_bytes=48 << 20),
    )(layer_early.T, layer_late)
    return sim[0, 0], share[0, :32], early_rows, late_rows


def solution(mesh):
    return jax.shard_map(
        body,
        mesh=mesh,
        in_specs=(P(None, ("gx", "gy")), P(("gx", "gy"), None)),
        out_specs=(P(), P(("gx", "gy")), P(("gx", "gy"), None), P(("gx", "gy"), None)),
        check_vma=False,
    )
```

time: 265 us -> 76.4 us (0.29)
  blocking collectives: 134 us -> 0 us
  Pallas kernels: 0 us -> 70.2 us
  waiting for transfers between devices: 63.8 us -> 0 us
  matrix products: 22.7 us -> 0 us
  starting transfers between devices: 15.7 us -> 0 us
  between operations: 17.3 us -> 1.82 us
  other arithmetic: 4.35 us -> 0 us
    psum x8 -> x0, blocking collectives: 85.5 us -> none  [one_axis_at_a_time(): return functools.reduce(lax.psum, axes, value)]
    pallas_call x0 -> x1, Pallas kernels: none -> 70.2 us  [body(): pl.pallas_call(kernel, out_shape=(jax.ShapeDtypeStruct((1, 128), F32), ja...]
    all_gather x1 -> x0, waiting for transfers between devices: 63.8 us -> none  [in_one_piece_2(): lax.all_gather(both, axis, axis=dim, tiled=True)]
    all_to_all x1 -> x0, blocking collectives: 48.4 us -> none  [from_everyone(): return lax.all_to_all(copies, axis, split_axis=0, concat_axis=0, tiled=True)]
    dot_general x2 -> x0, matrix products: 22.7 us -> none  [the longest x1 12.8 us: pair_terms(): lax.dot_general(left_early, right_early, dims, preferred_element_type=jnp...]
    all_to_all x2 -> x0, starting transfers between devices: 15.6 us -> none  [the longest x1 11.5 us: body(): lax.all_to_all(early_cols, GX_GY, split_axis=0, concat_axis=1, tiled=True)]
  transfers between devices with their start and end apart: 3 -> 0, of which waited for: 1 -> 0; matrix products, arithmetic and copies ran while one was open for 1% -> 0% of each run, Pallas kernels for 0% -> 0%
where the time goes in v1:
time: 76.4 us; the launch traced here: 76.2 us
  Pallas kernels  70.2 us (92%)
  local copies, waits for them, and re-layouts  4.18 us (5%)
  between operations  1.82 us (2%)
    pallas_call x1, Pallas kernels, body(): pl.pallas_call(kernel, out_shape=(jax.ShapeDtypeStruct((1, 128), F32), ja...  70.2 us
    unnamed x6, local copies, waits for them, and re-layouts  3.66 us

profile of v1, /device:TPU:1, one launch (start us, length us, event | category | flops | bytes accessed | tf_op | source)
XLA Modules:
  0.0 76.2 jit_solution(16269444921522060019)
XLA Ops:
  0.6 0.0 copy-start
  0.6 1.0 %copy-done = bf16[4096,64]{0,1:T(8,128)(2,1)S(1)} copy-done((bf16[4096,64]{0,1:T(8,128)(2,1)S(1)}, bf16[4096,64]{0,1:T(8,128)(2,1)}, u32[]{:S(2)}) %copy-start) | copy-done | bytes 524312
  1.7 0.0 copy-start.1
  1.7 1.0 %copy-done.1 = bf16[32,8192]{1,0:T(8,128)(2,1)S(1)} copy-done((bf16[32,8192]{1,0:T(8,128)(2,1)S(1)}, bf16[32,8192]{1,0:T(8,128)(2,1)}, u32[]{:S(2)}) %copy-start.1) | copy-done | bytes 524312
  2.7 70.2 %shard_map.57 = (f32[1,128]{1,0:T(1,128)S(1)}, f32[1,128]{1,0:T(1,128)S(1)}, bf16[32,8192]{1,0:T(8,128)(2,1)S(1)}, bf16[32,8192]{1,0:T(8,128)(2,1)S(1)}) custom-call(bf16[64,4096]{1,0:T(8,128)(2,1)S(1)} %bitcast.5, bf16[32,8192]{1,0:T(8,128)(2,1)S(1)} %copy-done.1), custom_call_target="tpu_custom_call" | custom-call | tf_op jit(solution)/shard_map/pallas_call | solution.py:443
  72.9 0.5 slice_bitcast_fusion
  73.5 0.8 %copy.10 = bf16[32,8192]{1,0:T(8,128)(2,1)} copy(bf16[32,8192]{1,0:T(8,128)(2,1)S(1)} %get-tuple-element.18) | data formatting | bytes 1048576
  74.3 0.8 %copy.11 = bf16[32,8192]{1,0:T(8,128)(2,1)} copy(bf16[32,8192]{1,0:T(8,128)(2,1)S(1)} %get-tuple-element.19) | data formatting | bytes 1048576
Async XLA Ops:
  0.6 1.0 %copy-start = (bf16[4096,64]{0,1:T(8,128)(2,1)S(1)}, bf16[4096,64]{0,1:T(8,128)(2,1)}, u32[]{:S(2)}) copy-start(bf16[4096,64]{0,1:T(8,128)(2,1)} %param.2) | copy-start | bytes 1572868
  1.7 1.0 %copy-start.1 = (bf16[32,8192]{1,0:T(8,128)(2,1)S(1)}, bf16[32,8192]{1,0:T(8,128)(2,1)}, u32[]{:S(2)}) copy-start(bf16[32,8192]{1,0:T(8,128)(2,1)} %late_hbm.1) | copy-start | bytes 1572868

commit v2 on v1

--- a/solution.py
+++ b/solution.py
@@ -25,6 +25,7 @@
 K_CORE = 1
 L_CORE = 0
 PIECES = 8
+ORDER = ((0, 0), (0, 1), (1, 0), (1, 1), (3, 0), (3, 1), (2, 0), (2, 1))
 
 
 def send(src, dst, send_sem, recv_sem, gx, gy):
@@ -104,10 +105,11 @@
     is_k = core == K_CORE
     is_l = core == L_CORE
 
-    def arrived(ref, sem):
-        pltpu.make_async_remote_copy(
-            src_ref=ref, dst_ref=ref, send_sem=sem, recv_sem=sem, device_id=(partner, z), device_id_type=MESH
-        ).wait_recv()
+    def arrived(ref, sem, name="wait"):
+        with jax.named_scope(name):
+            pltpu.make_async_remote_copy(
+                src_ref=ref, dst_ref=ref, send_sem=sem, recv_sem=sem, device_id=(partner, z), device_id_type=MESH
+            ).wait_recv()
 
     def left(ref, sem):
         pltpu.make_async_remote_copy(
@@ -120,6 +122,10 @@
     def level(dz):
         return lax.rem(z + dz, 4)
 
+    load_x = pltpu.make_async_copy(xt_hbm, xt, load_sem.at[0])
+    load_y = pltpu.make_async_copy(late_hbm, late, load_sem.at[1])
+    load_x.start()
+    load_y.start()
     barrier = pltpu.get_barrier_semaphore()
 
     @pl.loop(1, 16)
@@ -133,11 +139,8 @@
         pl.semaphore_signal(barrier, inc=1, device_id=(2 * chip + 1, level(dz)), device_id_type=MESH)
     pl.semaphore_signal(barrier, inc=1, device_id=(partner, z), device_id_type=MESH)
 
-    load_x = pltpu.make_async_copy(xt_hbm, xt, load_sem.at[0])
-    load_y = pltpu.make_async_copy(late_hbm, late, load_sem.at[1])
-    load_x.start()
-    load_y.start()
-    load_x.wait()
+    with jax.named_scope("load"):
+        load_x.wait()
 
     sums = jnp.zeros((64, 256), F32)
     for u in range(16):
@@ -147,16 +150,21 @@
         cen[u] = (xt[:, 256 * u : 256 * (u + 1)].astype(F32) - col_mean).astype(BF16)
     load_y.wait()
 
-    pl.semaphore_wait(barrier, 37)
+    with jax.named_scope("barrier"):
+        pl.semaphore_wait(barrier, 37)
+
+    def piece(j):
+        dz, q = ORDER[j]
+        return pl.ds(pl.multiple_of(32 * (4 * q + level(dz)), 32), 32)
 
     my_rows = pl.ds(pl.multiple_of(32 * (4 * core + z), 32), 32)
-    for dz in (1, 2, 3):
+    for dz in (1, 3, 2):
         to = level(dz)
         send(
             late.at[:, pl.ds(pl.multiple_of(2048 * to, 2048), 2048)],
             blocks.at[0, my_rows, :],
             late_send,
-            late_recv,
+            late_recv.at[2 * (4 - dz) + core],
             l_dev,
             to,
         )
@@ -165,25 +173,51 @@
     @pl.loop(1, 16)
     def _(r):
         other = lax.rem(chip + r, 16)
-        send(cen.at[other], rt.at[gx], early_send, early_recv, 2 * other + K_CORE, z)
+        send(cen.at[other], rt.at[gx], early_send, early_recv.at[x], 2 * other + K_CORE, z)
+
+    def forward(src, dst, j, ex, ey):
+        to = 2 * chip_at(4 - ex, 4 - ey) + core
+        rows = piece(j)
+        send(blocks.at[src, rows, :], blocks.at[dst, rows, :], gather_send, gather_recv.at[dst - 1, j], to, z)
+
+    def start(j):
+        forward(0, 1, j, 1, 0)
+        forward(0, 2, j, 0, 1)
 
     @pl.when(is_k)
     def _():
-        send(late.at[:, own_cols], blocks.at[0, my_rows, :], pair_send.at[0], late_recv, l_dev, z)
+        send(late.at[:, own_cols], blocks.at[0, my_rows, :], pair_send.at[0], late_recv.at[1], l_dev, z)
         rt[gx] = cen[chip]
-        arrived(rt.at[0:31], early_recv)
-
-        @pl.loop(0, 16)
-        def _(u):
-            cols = jnp.concatenate([rt[2 * u].astype(F32), rt[2 * u + 1].astype(F32)], axis=0)
-            at = pl.ds(pl.multiple_of(128 * u, 128), 128)
-            blocks[0, :, at] = cols.T.astype(BF16)
+        for dx in (0, 1, 3, 2):
+            xs = lax.rem(x + dx, 4)
+            arrived(rt.at[0 : 8 if dx else 7], early_recv.at[xs], f"w_early{dx}")
+
+            @pl.loop(0, 4)
+            def _(k):
+                u = 4 * xs + k
+                cols = jnp.concatenate([rt[2 * u].astype(F32), rt[2 * u + 1].astype(F32)], axis=0)
+                at = pl.ds(pl.multiple_of(128 * u, 128), 128)
+                blocks[0, :, at] = cols.T.astype(BF16)
+
+        for j in range(PIECES):
+            start(j)
+        for dz in (1, 2, 3):
+            for q in (0, 1):
+                rows = pl.ds(pl.multiple_of(32 * (4 * q + level(dz)), 32), 32)
+                send(blocks.at[0, rows, :], early_pieces.at[z], rows_send, rows_recv, 2 * chip + q, level(dz))
+        rows = pl.ds(pl.multiple_of(32 * (4 * L_CORE + z), 32), 32)
+        send(blocks.at[0, rows, :], early_pieces.at[z], pair_send.at[1], rows_recv, l_dev, z)
+        early_pieces[z] = blocks[0, my_rows, :]
 
     @pl.when(is_l)
     def _():
-        send(cen.at[chip], rt.at[gx], pair_send.at[0], early_recv, k_dev, z)
+        send(cen.at[chip], rt.at[gx], pair_send.at[0], early_recv.at[x], k_dev, z)
         blocks[0, my_rows, :] = late[:, own_cols]
-        arrived(blocks.at[0, 0:224, :], late_recv)
+        for j in range(PIECES):
+            if j:
+                arrived(blocks.at[0, piece(j), :], late_recv.at[2 * ORDER[j][0] + ORDER[j][1]], f"w_late{j}")
+            if j < 6:
+                start(j)
         for c in range(4):
             at = slice(512 * c, 512 * (c + 1))
             part = jnp.zeros((32, 512), F32)
@@ -197,50 +231,38 @@
             other = lax.rem(chip + r, 16)
             send(own_sum, plane_sums.at[chip], sums_send, sums_recv, 2 * other + L_CORE, z)
 
-        arrived(plane_sums.at[0:15], sums_recv)
+        start(6)
+        start(7)
+
+    def center(slot):
+        for c in range(4):
+            at = slice(512 * c, 512 * (c + 1))
+            m = mean_out[:, at]
+            for r in range(8):
+                rows = slice(32 * r, 32 * (r + 1))
+                blocks[6 + slot, rows, at] = (blocks[slot, rows, at].astype(F32) - m).astype(BF16)
+
+    def late_mean():
+        arrived(plane_sums.at[0:15], sums_recv, "w_sums")
         mean = plane_sums[0]
         for u in range(1, 16):
             mean = mean + plane_sums[u]
         mean_out[...] = mean / 4096.0
         means[z] = mean_out[...]
-        for c in range(4):
-            at = slice(512 * c, 512 * (c + 1))
-            m = mean_out[:, at]
-            for r in range(8):
-                rows = slice(32 * r, 32 * (r + 1))
-                blocks[0, rows, at] = (blocks[0, rows, at].astype(F32) - m).astype(BF16)
-
-    def forward(src, dst, piece, ex, ey):
-        rows = pl.ds(32 * piece, 32)
-        to = 2 * chip_at(4 - ex, 4 - ey) + core
-        send(blocks.at[src, rows, :], blocks.at[dst, rows, :], gather_send, gather_recv.at[dst - 1, piece], to, z)
-
-    for i in range(PIECES):
-        forward(0, 1, i, 1, 0)
-        forward(0, 2, i, 0, 1)
-
-    @pl.when(is_l)
-    def _():
         send(mean_out, means.at[z], pair_send.at[1], mean_recv, k_dev, z)
         for dz in (1, 2, 3):
             send(mean_out, means.at[z], mean_send, mean_recv, k_dev, level(dz))
             send(mean_out, means.at[z], mean_send, mean_recv, l_dev, level(dz))
-
-    @pl.when(is_k)
-    def _():
-        for dz in (1, 2, 3):
-            for q in (0, 1):
-                rows = pl.ds(pl.multiple_of(32 * (4 * q + level(dz)), 32), 32)
-                send(blocks.at[0, rows, :], early_pieces.at[z], rows_send, rows_recv, 2 * chip + q, level(dz))
-        rows = pl.ds(pl.multiple_of(32 * (4 * L_CORE + z), 32), 32)
-        send(blocks.at[0, rows, :], early_pieces.at[z], pair_send.at[1], rows_recv, l_dev, z)
-        early_pieces[z] = blocks[0, my_rows, :]
+        center(0)
 
     dims = (((1,), (1,)), ((), ()))
+
+    ready = 6 * (1 - core)
 
     def product(t):
         a, b, _ = TILES[t]
-        gram[t] = lax.dot_general(blocks[a], blocks[b], dims, preferred_element_type=F32)
+        with jax.named_scope(f"dot{t}"):
+            gram[t] = lax.dot_general(blocks[a + ready], blocks[b + ready], dims, preferred_element_type=F32)
         if t > 0:
             stage[t - 1] = gram[t].astype(BF16)
         for dz in (1, 2, 3):
@@ -266,10 +288,10 @@
         _, b, both = TILES[t]
         rows = pl.ds(pl.multiple_of(64 * z, 64), 64)
         if t == 0:
-            arrived(parts0, part0_recv)
+            arrived(parts0, part0_recv, "wp0")
             get = lambda s: parts0[s]
         else:
-            arrived(parts.at[t - 1], part_recv.at[t - 1])
+            arrived(parts.at[t - 1], part_recv.at[t - 1], f"wp{t}")
             get = lambda s: parts[t - 1, s].astype(F32)
         k = gram[t, rows, :] + ((get(0) + get(1)) + get(2))
         l = (get(3) + get(4)) + (get(5) + get(6))
@@ -283,36 +305,41 @@
         acc[1] += weight * (l * l)
         acc[2] += weight * h
 
-    product(0)
-
     @pl.when(is_k)
     def _():
         acc[...] = jnp.zeros_like(acc)
         row_cols[...] = jnp.zeros_like(row_cols)
         col_acc[...] = jnp.zeros_like(col_acc)
 
-    for i in range(PIECES):
-        rows = slice(32 * i, 32 * (i + 1))
-        arrived(blocks.at[1, rows, :], gather_recv.at[0, i])
-        forward(1, 4, i, 0, 3)
-        arrived(blocks.at[2, rows, :], gather_recv.at[1, i])
-        forward(2, 5, i, 3, 0)
-        rows = pl.ds(32 * i, 32)
+    for j in range(PIECES):
+        rows = piece(j)
+        arrived(blocks.at[1, rows, :], gather_recv.at[0, j], f"w1_{j}")
+        forward(1, 4, j, 0, 3)
+        arrived(blocks.at[2, rows, :], gather_recv.at[1, j], f"w2_{j}")
+        forward(2, 5, j, 3, 0)
         to = 2 * chip_at(4 - (1 - core), 4 - core) + core
-        send(blocks.at[2 - core, rows, :], blocks.at[3, rows, :], gather_send, gather_recv.at[2, i], to, z)
+        send(blocks.at[2 - core, rows, :], blocks.at[3, rows, :], gather_send, gather_recv.at[2, j], to, z)
+        if j == 4:
+            pl.when(is_l)(late_mean)
+            product(0)
+
+    @pl.when(is_l)
+    def _():
+        center(1)
+        center(2)
 
     for t in (1, 2, 3):
         product(t)
 
     @pl.when(is_k)
     def _():
-        arrived(means, mean_recv)
-        arrived(early_pieces.at[0:3], rows_recv)
+        arrived(means, mean_recv, "w_mean")
+        arrived(early_pieces.at[0:3], rows_recv, "w_rows")
 
     @pl.when(is_l)
     def _():
-        arrived(means.at[0:3], mean_recv)
-        arrived(early_pieces, rows_recv)
+        arrived(means.at[0:3], mean_recv, "w_mean")
+        arrived(early_pieces, rows_recv, "w_rows")
 
     for c in range(4):
         at = slice(2048 * c, 2048 * (c + 1))
@@ -331,11 +358,14 @@
     put_e.start()
     put_l.start()
 
-    for i in range(PIECES):
-        arrived(blocks.at[4, 32 * i : 32 * (i + 1), :], gather_recv.at[3, i])
+    def take(slot):
+        for j in range(PIECES):
+            arrived(blocks.at[slot, piece(j), :], gather_recv.at[slot - 1, j], f"w{slot}_{j}")
+        pl.when(is_l)(lambda: center(slot))
+
+    take(4)
     product(4)
-    for i in range(PIECES):
-        arrived(blocks.at[5, 32 * i : 32 * (i + 1), :], gather_recv.at[4, i])
+    take(5)
     product(5)
     product(6)
 
@@ -344,8 +374,7 @@
         for t in (0, 1, 2, 3):
             settle(t)
 
-    for i in range(PIECES):
-        arrived(blocks.at[3, 32 * i : 32 * (i + 1), :], gather_recv.at[2, i])
+    take(3)
     for t in (7, 8, 9):
         product(t)
 
@@ -380,7 +409,7 @@
                 if r:
                     send(msg.at[r], msg_in.at[r], msg_send, msg_recv, 2 * chip_at(dx, dy) + K_CORE, z)
         msg_in[0] = msg[0]
-        arrived(msg_in.at[0:15], msg_recv)
+        arrived(msg_in.at[0:15], msg_recv, "w_msg")
         s = msg_in[0]
         for r in range(1, 16):
             s = s + msg_in[r]
@@ -390,11 +419,11 @@
             send(total, total_in.at[dz - 1], total_send, total_recv, l_dev, level(dz))
         send(total, total_in.at[3], pair_send.at[2], total_recv, l_dev, z)
         total_in[3] = total[...]
-        arrived(total_in.at[0:3], total_recv)
+        arrived(total_in.at[0:3], total_recv, "w_tot")
 
     @pl.when(is_l)
     def _():
-        arrived(total_in, total_recv)
+        arrived(total_in, total_recv, "w_tot")
 
     final = (total_in[0] + total_in[1]) + (total_in[2] + total_in[3])
     scal_lane = lax.broadcasted_iota(jnp.int32, (1, 128), 1)
@@ -408,7 +437,8 @@
         tokens = jnp.where(z == j, pltpu.roll(half, 128 - 32 * j, 1), tokens)
     share_ref[...] = 4096.0 * tokens / norm
 
-    put_e.wait()
+    with jax.named_scope("end"):
+        put_e.wait()
     put_l.wait()
     left(late.at[:, 0:6144], late_send)
     left(cen.at[0:15], early_send)
@@ -433,6 +463,33 @@
         left(parts.at[:, 0], pair_send.at[3])
         left(plane_sums.at[0:15], sums_send)
         left(plane_sums.at[0:6], mean_send)
+
+
+CHUNKS = 4
+
+
+def publish(share_in, sim_in, early_in, late_in, share, sim, early, late, bufs, in_sem, out_sem):
+    width = 8192 // CHUNKS
+    moves = []
+    for k, (src, dst) in enumerate(((early_in, early), (late_in, late))):
+        for c in range(CHUNKS):
+            at = pl.ds(width * c, width)
+            n = CHUNKS * k + c
+            moves.append(
+                (
+                    pltpu.make_async_copy(src.at[:, at], bufs.at[n], in_sem.at[n]),
+                    pltpu.make_async_copy(bufs.at[n], dst.at[:, at], out_sem.at[n]),
+                )
+            )
+    for get, _ in moves:
+        get.start()
+    share[...] = share_in[:, 0:32]
+    sim[...] = sim_in[:, 0:1]
+    for get, put in moves:
+        get.wait()
+        put.start()
+    for _, put in moves:
+        put.wait()
 
 
 def body(layer_early, layer_late):
@@ -455,7 +512,7 @@
             vm((32, 8192), BF16),
             vm((16, 64, 256), BF16),
             vm((32, 64, 256), BF16),
-            vm((6, 256, 2048), BF16),
+            vm((12, 256, 2048), BF16),
             vm((10, 256, 256), F32),
             vm((9, 256, 256), BF16),
             vm((9, 7, 64, 256), BF16),
@@ -477,10 +534,10 @@
             dma((2,)),
             dma((2,)),
             dma,
-            dma,
-            dma,
+            dma((8,)),
             dma,
             dma((4,)),
+            dma((4,)),
             dma,
             dma,
             dma,
@@ -498,9 +555,21 @@
             dma,
             dma,
         ],
-        compiler_params=pltpu.CompilerParams(collective_id=0, has_side_effects=True, vmem_limit_bytes=48 << 20),
+        compiler_params=pltpu.CompilerParams(collective_id=0, has_side_effects=True, vmem_limit_bytes=67043328),
     )(layer_early.T, layer_late)
-    return sim[0, 0], share[0, :32], early_rows, late_rows
+    share, sim, early_rows, late_rows = pl.pallas_call(
+        publish,
+        out_shape=(
+            jax.ShapeDtypeStruct((1, 32), F32),
+            jax.ShapeDtypeStruct((1, 1), F32),
+            jax.ShapeDtypeStruct((32, 8192), BF16),
+            jax.ShapeDtypeStruct((32, 8192), BF16),
+        ),
+        in_specs=[whole, whole, hbm, hbm],
+        out_specs=(whole, whole, hbm, hbm),
+        scratch_shapes=[vm((2 * CHUNKS, 32, 8192 // CHUNKS), BF16), dma((2 * CHUNKS,)), dma((2 * CHUNKS,))],
+    )(share, sim, early_rows, late_rows)
+    return sim.reshape(()), share.reshape(32), early_rows, late_rows
 
 
 def solution(mesh):

time: 76.4 us -> 70.6 us (0.924)
  local copies, waits for them, and re-layouts: 4.18 us -> 0 us
  between operations: 1.82 us -> 0.64 us
    unnamed x6 -> x0, local copies, waits for them, and re-layouts: 3.66 us -> none
    pallas_call x1, Pallas kernels: 70.2 us -> 66.5 us  [body(): pl.pallas_call(kernel, out_shape=(jax.ShapeDtypeStruct((1, 128), F32), ja...]
    pallas_call x0 -> x1, Pallas kernels: none -> 3.27 us  [body(): pl.pallas_call(publish, out_shape=(jax.ShapeDtypeStruct((1, 32), F32), ja...]
where the time goes in v2:
time: 70.6 us; the launch traced here: 70.5 us
  Pallas kernels  69.8 us (99%)
    pallas_call x1, Pallas kernels, body(): pl.pallas_call(kernel, out_shape=(jax.ShapeDtypeStruct((1, 128), F32), ja...  66.5 us
    pallas_call x1, Pallas kernels, body(): pl.pallas_call(publish, out_shape=(jax.ShapeDtypeStruct((1, 32), F32), ja...  3.27 us

profile of v2, /device:TPU:1, one launch (start us, length us, event | category | flops | bytes accessed | tf_op | source)
XLA Modules:
  0.0 70.5 jit_solution(9598566573162262528)
XLA Ops:
  0.6 66.5 %shard_map.57 = (f32[1,128]{1,0:T(1,128)}, f32[1,128]{1,0:T(1,128)}, bf16[32,8192]{1,0:T(8,128)(2,1)}, bf16[32,8192]{1,0:T(8,128)(2,1)}) custom-call(bf16[64,4096]{1,0:T(8,128)(2,1)} %bitcast.3, bf16[32,8192]{1,0:T(8,128)(2,1)} %late_hbm.1), custom_call_target="tpu_custom_call" | custom-call | tf_op jit(solution)/shard_map/pallas_call | solution.py:500
  67.2 3.3 %shard_map.58 = (f32[1,32]{1,0:T(1,128)}, f32[1,1]{1,0:T(1,128)}, bf16[32,8192]{1,0:T(8,128)(2,1)}, bf16[32,8192]{1,0:T(8,128)(2,1)}) custom-call(f32[1,128]{1,0:T(1,128)} %get-tuple-element.12.share_in, f32[1,128]{1,0:T(1,128)} %get-tuple-element.13.sim_in, bf16[32,8192]{1,0:T(8,128)(2,1)} %get-tuple-element.14.early_in, ...), custom_call_target="tpu_custom_call" | custom-call | tf_op jit(solution)/shard_map/pallas_call | solution.py:560

commit v3 on v2

--- a/solution.py
+++ b/solution.py
@@ -254,6 +254,7 @@
             send(mean_out, means.at[z], mean_send, mean_recv, k_dev, level(dz))
             send(mean_out, means.at[z], mean_send, mean_recv, l_dev, level(dz))
         center(0)
+        product(0)
 
     dims = (((1,), (1,)), ((), ()))
 
@@ -311,17 +312,19 @@
         row_cols[...] = jnp.zeros_like(row_cols)
         col_acc[...] = jnp.zeros_like(col_acc)
 
+        product(0)
+
     for j in range(PIECES):
         rows = piece(j)
         arrived(blocks.at[1, rows, :], gather_recv.at[0, j], f"w1_{j}")
         forward(1, 4, j, 0, 3)
         arrived(blocks.at[2, rows, :], gather_recv.at[1, j], f"w2_{j}")
         forward(2, 5, j, 3, 0)
-        to = 2 * chip_at(4 - (1 - core), 4 - core) + core
-        send(blocks.at[2 - core, rows, :], blocks.at[3, rows, :], gather_send, gather_recv.at[2, j], to, z)
-        if j == 4:
+        if j == 6:
             pl.when(is_l)(late_mean)
-            product(0)
+
+    for j in range(PIECES):
+        forward(2 - core, 3, j, 1 - core, core)
 
     @pl.when(is_l)
     def _():

time: 70.6 us -> 72.3 us (1.024)
  Pallas kernels: 69.8 us -> 71.4 us
    pallas_call x1, Pallas kernels: 66.5 us -> 68.2 us  [body(): pl.pallas_call(kernel, out_shape=(jax.ShapeDtypeStruct((1, 128), F32), ja...]
where the time goes in v3:
time: 72.3 us; the launch traced here: 72.1 us
  Pallas kernels  71.4 us (99%)
    pallas_call x1, Pallas kernels, body(): pl.pallas_call(kernel, out_shape=(jax.ShapeDtypeStruct((1, 128), F32), ja...  68.2 us
    pallas_call x1, Pallas kernels, body(): pl.pallas_call(publish, out_shape=(jax.ShapeDtypeStruct((1, 32), F32), ja...  3.27 us

profile of v3, /device:TPU:1, one launch (start us, length us, event | category | flops | bytes accessed | tf_op | source)
XLA Modules:
  0.0 72.1 jit_solution(8756334348241893280)
XLA Ops:
  0.6 68.2 %shard_map.57 = (f32[1,128]{1,0:T(1,128)}, f32[1,128]{1,0:T(1,128)}, bf16[32,8192]{1,0:T(8,128)(2,1)}, bf16[32,8192]{1,0:T(8,128)(2,1)}) custom-call(bf16[64,4096]{1,0:T(8,128)(2,1)} %bitcast.3, bf16[32,8192]{1,0:T(8,128)(2,1)} %late_hbm.1), custom_call_target="tpu_custom_call" | custom-call | tf_op jit(solution)/shard_map/pallas_call | solution.py:503
  68.8 3.3 %shard_map.58 = (f32[1,32]{1,0:T(1,128)}, f32[1,1]{1,0:T(1,128)}, bf16[32,8192]{1,0:T(8,128)(2,1)}, bf16[32,8192]{1,0:T(8,128)(2,1)}) custom-call(f32[1,128]{1,0:T(1,128)} %get-tuple-element.12.share_in, f32[1,128]{1,0:T(1,128)} %get-tuple-element.13.sim_in, bf16[32,8192]{1,0:T(8,128)(2,1)} %get-tuple-element.14.early_in, ...), custom_call_target="tpu_custom_call" | custom-call | tf_op jit(solution)/shard_map/pallas_call | solution.py:563

commit v4 on v3

--- a/solution.py
+++ b/solution.py
@@ -10,18 +10,8 @@
 BF16 = jnp.bfloat16
 
 SLOTS = ((0, 0), (1, 0), (0, 1), (1, 1), (1, 3), (3, 1))
-TILES = (
-    (0, 0, False),
-    (1, 0, True),
-    (2, 0, True),
-    (1, 2, True),
-    (4, 2, True),
-    (5, 1, True),
-    (4, 5, False),
-    (3, 0, True),
-    (3, 5, False),
-    (4, 3, False),
-)
+TILES = ((0, 0), (1, 0), (2, 0), (1, 2), (4, 2), (5, 1), (3, 0), (4, 5), (3, 5), (3, 4))
+SHARED = 7
 K_CORE = 1
 L_CORE = 0
 PIECES = 8
@@ -54,6 +44,8 @@
     gram,
     stage,
     parts,
+    halves,
+    half_parts,
     parts0,
     own_sum,
     plane_sums,
@@ -64,6 +56,7 @@
     late_out,
     acc,
     row_cols,
+    half_cols,
     col_acc,
     msg,
     msg_in,
@@ -86,6 +79,7 @@
     rows_recv,
     part_send,
     part_recv,
+    half_send,
     part0_send,
     part0_recv,
     msg_send,
@@ -128,8 +122,7 @@
     load_y.start()
     barrier = pltpu.get_barrier_semaphore()
 
-    @pl.loop(1, 16)
-    def _(r):
+    for r in range(1, 16):
         other = lax.rem(chip + r, 16)
         pl.semaphore_signal(barrier, inc=1, device_id=(2 * other, z), device_id_type=MESH)
         pl.semaphore_signal(barrier, inc=1, device_id=(2 * other + 1, z), device_id_type=MESH)
@@ -260,56 +253,78 @@
 
     ready = 6 * (1 - core)
 
+    def sides(t):
+        a, b = TILES[t]
+        if t < SHARED:
+            return a, b, 0
+        half = (y if t == 9 else x) // 2
+        return a + half * (b - a), b + half * (a - b), half
+
     def product(t):
-        a, b, _ = TILES[t]
+        a, b, half = sides(t)
         with jax.named_scope(f"dot{t}"):
-            gram[t] = lax.dot_general(blocks[a + ready], blocks[b + ready], dims, preferred_element_type=F32)
-        if t > 0:
+            if t < SHARED:
+                gram[t] = lax.dot_general(blocks[a + ready], blocks[b + ready], dims, preferred_element_type=F32)
+            else:
+                top = pl.ds(pl.multiple_of(128 * half, 128), 128)
+                gram[t, 0:128, :] = lax.dot_general(
+                    blocks[a + ready, top, :], blocks[b + ready], dims, preferred_element_type=F32
+                )
+        if t == 0:
+            src, dst, size, out, into, pair = gram.at[0], parts0, 64, part0_send, part0_recv, 2
+        elif t < SHARED:
+            src, dst, size, out, into, pair = stage.at[t - 1], parts.at[t - 1], 64, part_send, part_recv.at[t - 1], 3
             stage[t - 1] = gram[t].astype(BF16)
+        else:
+            n = t - SHARED
+            src, dst, size, out, into, pair = halves.at[n], half_parts.at[n], 32, half_send, part_recv.at[t - 1], 4
+            halves[n] = gram[t, 0:128, :].astype(BF16)
         for dz in (1, 2, 3):
             to = level(dz)
-            rows = pl.ds(pl.multiple_of(64 * to, 64), 64)
-            slot = dz - 1 + 4 * (1 - core)
-            if t == 0:
-                send(gram.at[0, rows, :], parts0.at[slot], part0_send, part0_recv, k_dev, to)
-            else:
-                send(stage.at[t - 1, rows, :], parts.at[t - 1, slot], part_send, part_recv.at[t - 1], k_dev, to)
+            rows = pl.ds(pl.multiple_of(size * to, size), size)
+            send(src.at[rows, :], dst.at[dz - 1 + 4 * (1 - core)], out, into, k_dev, to)
 
         @pl.when(is_l)
         def _():
-            rows = pl.ds(pl.multiple_of(64 * z, 64), 64)
-            if t == 0:
-                send(gram.at[0, rows, :], parts0.at[3], pair_send.at[2], part0_recv, k_dev, z)
-            else:
-                send(stage.at[t - 1, rows, :], parts.at[t - 1, 3], pair_send.at[3], part_recv.at[t - 1], k_dev, z)
-
-    lane = lax.broadcasted_iota(jnp.int32, (64, 128), 1)
+            rows = pl.ds(pl.multiple_of(size * z, size), size)
+            send(src.at[rows, :], dst.at[3], pair_send.at[pair], into, k_dev, z)
 
     def settle(t):
-        _, b, both = TILES[t]
-        rows = pl.ds(pl.multiple_of(64 * z, 64), 64)
+        _, b, _ = sides(t)
         if t == 0:
-            arrived(parts0, part0_recv, "wp0")
-            get = lambda s: parts0[s]
+            size, buf, sem = 64, parts0, part0_recv
+        elif t < SHARED:
+            size, buf, sem = 64, parts.at[t - 1], part_recv.at[t - 1]
         else:
-            arrived(parts.at[t - 1], part_recv.at[t - 1], f"wp{t}")
-            get = lambda s: parts[t - 1, s].astype(F32)
-        k = gram[t, rows, :] + ((get(0) + get(1)) + get(2))
-        l = (get(3) + get(4)) + (get(5) + get(6))
+            size, buf, sem = 32, half_parts.at[t - SHARED], part_recv.at[t - 1]
+        arrived(buf, sem, f"wp{t}")
+        part = [buf[n].astype(F32) for n in range(7)]
+        rows = pl.ds(pl.multiple_of(size * z, size), size)
+        k = gram[t, rows, :] + ((part[0] + part[1]) + part[2])
+        l = (part[3] + part[4]) + (part[5] + part[6])
         h = k * l
-        row_cols[...] += jnp.where(lane == t, jnp.sum(h, axis=1, keepdims=True), 0.0)
+        lane = lax.broadcasted_iota(jnp.int32, (size, 128), 1)
+        own = jnp.where(lane == t, jnp.sum(h, axis=1, keepdims=True), 0.0)
         weight = 1.0
-        if both:
+        if t:
             weight = 2.0
-            col_acc[b : b + 1, :] += jnp.sum(h, axis=0, keepdims=True)
-        acc[0] += weight * (k * k)
-        acc[1] += weight * (l * l)
-        acc[2] += weight * h
+            across = jnp.sum(h, axis=0, keepdims=True)
+            col_acc[...] += jnp.where(slot_row == b, across, 0.0)
+        if t < SHARED:
+            row_cols[...] += own
+        else:
+            half_cols[...] += own
+        acc[0, 0:size] += weight * (k * k)
+        acc[1, 0:size] += weight * (l * l)
+        acc[2, 0:size] += weight * h
+
+    slot_row = lax.broadcasted_iota(jnp.int32, (8, 256), 0)
 
     @pl.when(is_k)
     def _():
         acc[...] = jnp.zeros_like(acc)
         row_cols[...] = jnp.zeros_like(row_cols)
+        half_cols[...] = jnp.zeros_like(half_cols)
         col_acc[...] = jnp.zeros_like(col_acc)
 
         product(0)
@@ -320,11 +335,14 @@
         forward(1, 4, j, 0, 3)
         arrived(blocks.at[2, rows, :], gather_recv.at[1, j], f"w2_{j}")
         forward(2, 5, j, 3, 0)
+        pl.when(is_k)(lambda: forward(1, 3, j, 0, 1))
         if j == 6:
             pl.when(is_l)(late_mean)
 
-    for j in range(PIECES):
-        forward(2 - core, 3, j, 1 - core, core)
+    @pl.when(is_l)
+    def _():
+        for j in range(PIECES):
+            forward(2, 3, j, 1, 0)
 
     @pl.when(is_l)
     def _():
@@ -370,7 +388,7 @@
     product(4)
     take(5)
     product(5)
-    product(6)
+    product(7)
 
     @pl.when(is_k)
     def _():
@@ -378,16 +396,24 @@
             settle(t)
 
     take(3)
-    for t in (7, 8, 9):
+    for t in (6, 8, 9):
         product(t)
 
     @pl.when(is_k)
     def _():
-        for t in (4, 5, 6, 7, 8, 9):
+        for t in (4, 5, 7, 6, 8, 9):
             settle(t)
-        sides = row_cols[...]
-        turned = jnp.concatenate([sides] * 4, axis=0).T
-        mine = lax.broadcasted_iota(jnp.int32, (1, 256), 1) // 64 == z
+        turned = jnp.concatenate([row_cols[...]] * 4, axis=0).T
+        half_turned = jnp.concatenate([half_cols[...]] * 8, axis=0).T
+        col = lax.broadcasted_iota(jnp.int32, (1, 256), 1)
+        both = col_acc[...]
+        for t in range(len(TILES)):
+            a, _, half = sides(t)
+            if t < SHARED:
+                row = jnp.where(col // 64 == z, turned[t : t + 1, :], 0.0)
+            else:
+                row = jnp.where(col // 32 == 4 * half + z, half_turned[t : t + 1, :], 0.0)
+            both = both + jnp.where(slot_row == a, row, 0.0)
         scal_lane = lax.broadcasted_iota(jnp.int32, (1, 128), 1)
         scal = jnp.zeros((1, 128), F32)
         for j in range(3):
@@ -398,11 +424,7 @@
                 r = 4 * dx + dy
                 if (dx, dy) in SLOTS:
                     slot = SLOTS.index((dx, dy))
-                    row = jnp.zeros((1, 256), F32)
-                    for t, (a, _, _) in enumerate(TILES):
-                        if a == slot:
-                            row = row + turned[t : t + 1, :]
-                    msg[r, :, 0:256] = col_acc[slot : slot + 1, :] + jnp.where(mine, row, 0.0)
+                    msg[r, :, 0:256] = both[slot : slot + 1, :]
                 else:
                     msg[r, :, 0:256] = jnp.zeros((1, 256), F32)
                 msg[r, :, 256:384] = scal
@@ -433,12 +455,12 @@
     scal = final[:, 256:384]
     kk, ll, kl = (jnp.sum(jnp.where(scal_lane == j, scal, 0.0), axis=1, keepdims=True) for j in range(3))
     norm = jnp.sqrt(kk * ll)
-    sim_ref[...] = jnp.broadcast_to(kl / norm, (1, 128))
+    sim_ref[...] = kl / norm
     half = jnp.where(core == 0, final[:, 0:128], final[:, 128:256])
     tokens = half
     for j in (1, 2, 3):
         tokens = jnp.where(z == j, pltpu.roll(half, 128 - 32 * j, 1), tokens)
-    share_ref[...] = 4096.0 * tokens / norm
+    share_ref[...] = (4096.0 * tokens / norm)[:, 0:32]
 
     with jax.named_scope("end"):
         put_e.wait()
@@ -447,6 +469,7 @@
     left(cen.at[0:15], early_send)
     left(blocks.at[1:6], gather_send)
     left(parts.at[:, 0:3], part_send)
+    left(half_parts.at[:, 0:3], half_send)
     left(parts0.at[0:3], part0_send)
 
     @pl.when(is_k)
@@ -464,6 +487,7 @@
         left(mean_out, pair_send.at[1])
         left(parts0.at[0], pair_send.at[2])
         left(parts.at[:, 0], pair_send.at[3])
+        left(half_parts.at[:, 0], pair_send.at[4])
         left(plane_sums.at[0:15], sums_send)
         left(plane_sums.at[0:6], mean_send)
 
@@ -471,27 +495,21 @@
 CHUNKS = 4
 
 
-def publish(share_in, sim_in, early_in, late_in, share, sim, early, late, bufs, in_sem, out_sem):
+def publish(share_in, sim_in, early_in, late_in, share, sim, early, late, bufs, share_buf, sim_buf, in_sem, out_sem):
     width = 8192 // CHUNKS
-    moves = []
+    ways = [(share_in, share_buf, share), (sim_in, sim_buf, sim)]
     for k, (src, dst) in enumerate(((early_in, early), (late_in, late))):
         for c in range(CHUNKS):
             at = pl.ds(width * c, width)
-            n = CHUNKS * k + c
-            moves.append(
-                (
-                    pltpu.make_async_copy(src.at[:, at], bufs.at[n], in_sem.at[n]),
-                    pltpu.make_async_copy(bufs.at[n], dst.at[:, at], out_sem.at[n]),
-                )
-            )
-    for get, _ in moves:
+            ways.append((src.at[:, at], bufs.at[CHUNKS * k + c], dst.at[:, at]))
+    gets = [pltpu.make_async_copy(a, b, in_sem.at[n]) for n, (a, b, _) in enumerate(ways)]
+    puts = [pltpu.make_async_copy(b, c, out_sem.at[n]) for n, (_, b, c) in enumerate(ways)]
+    for get in gets:
         get.start()
-    share[...] = share_in[:, 0:32]
-    sim[...] = sim_in[:, 0:1]
-    for get, put in moves:
+    for get, put in zip(gets, puts):
         get.wait()
         put.start()
-    for _, put in moves:
+    for put in puts:
         put.wait()
 
 
@@ -503,8 +521,8 @@
     share, sim, early_rows, late_rows = pl.pallas_call(
         kernel,
         out_shape=(
-            jax.ShapeDtypeStruct((1, 128), F32),
-            jax.ShapeDtypeStruct((1, 128), F32),
+            jax.ShapeDtypeStruct((1, 32), F32),
+            jax.ShapeDtypeStruct((1, 1), F32),
             jax.ShapeDtypeStruct((32, 8192), BF16),
             jax.ShapeDtypeStruct((32, 8192), BF16),
         ),
@@ -517,8 +535,10 @@
             vm((32, 64, 256), BF16),
             vm((12, 256, 2048), BF16),
             vm((10, 256, 256), F32),
-            vm((9, 256, 256), BF16),
-            vm((9, 7, 64, 256), BF16),
+            vm((6, 256, 256), BF16),
+            vm((6, 7, 64, 256), BF16),
+            vm((3, 128, 256), BF16),
+            vm((3, 7, 32, 256), BF16),
             vm((7, 64, 256), F32),
             vm((1, 2048), F32),
             vm((16, 1, 2048), F32),
@@ -529,6 +549,7 @@
             vm((32, 8192), BF16),
             vm((3, 64, 256), F32),
             vm((64, 128), F32),
+            vm((32, 128), F32),
             vm((8, 256), F32),
             vm((16, 1, 384), F32),
             vm((16, 1, 384), F32),
@@ -540,7 +561,7 @@
             dma((8,)),
             dma,
             dma((4,)),
-            dma((4,)),
+            dma((5,)),
             dma,
             dma,
             dma,
@@ -551,6 +572,7 @@
             dma,
             dma,
             dma((9,)),
+            dma,
             dma,
             dma,
             dma,
@@ -568,9 +590,15 @@
             jax.ShapeDtypeStruct((32, 8192), BF16),
             jax.ShapeDtypeStruct((32, 8192), BF16),
         ),
-        in_specs=[whole, whole, hbm, hbm],
-        out_specs=(whole, whole, hbm, hbm),
-        scratch_shapes=[vm((2 * CHUNKS, 32, 8192 // CHUNKS), BF16), dma((2 * CHUNKS,)), dma((2 * CHUNKS,))],
+        in_specs=[hbm] * 4,
+        out_specs=(hbm,) * 4,
+        scratch_shapes=[
+            vm((2 * CHUNKS, 32, 8192 // CHUNKS), BF16),
+            vm((1, 32), F32),
+            vm((1, 1), F32),
+            dma((2 * CHUNKS + 2,)),
+            dma((2 * CHUNKS + 2,)),
+        ],
     )(share, sim, early_rows, late_rows)
     return sim.reshape(()), share.reshape(32), early_rows, late_rows
 

time: 72.3 us -> 68.1 us (0.942)
  Pallas kernels: 71.4 us -> 67.3 us
    pallas_call x1, Pallas kernels: 68.2 us -> 64.6 us  [body(): pl.pallas_call(kernel, out_shape=(jax.ShapeDtypeStruct((1, 32), F32), jax...]
where the time goes in v4:
time: 68.1 us; the launch traced here: 68 us
  Pallas kernels  67.3 us (99%)
    pallas_call x1, Pallas kernels, body(): pl.pallas_call(kernel, out_shape=(jax.ShapeDtypeStruct((1, 32), F32), jax...  64.6 us
    pallas_call x1, Pallas kernels, body(): pl.pallas_call(publish, out_shape=(jax.ShapeDtypeStruct((1, 32), F32), ja...  2.76 us

profile of v4, /device:TPU:1, one launch (start us, length us, event | category | flops | bytes accessed | tf_op | source)
XLA Modules:
  0.0 68.0 jit_solution(11857317831029661035)
XLA Ops:
  0.6 64.6 %shard_map.57 = (f32[1,32]{1,0:T(1,128)}, f32[1,1]{1,0:T(1,128)}, bf16[32,8192]{1,0:T(8,128)(2,1)}, bf16[32,8192]{1,0:T(8,128)(2,1)}) custom-call(bf16[64,4096]{1,0:T(8,128)(2,1)} %bitcast.3, bf16[32,8192]{1,0:T(8,128)(2,1)} %late_hbm.1), custom_call_target="tpu_custom_call" | custom-call | tf_op jit(solution)/shard_map/pallas_call | solution.py:521
  65.2 2.8 %shard_map.58 = (f32[1,32]{1,0:T(1,128)}, f32[1,1]{1,0:T(1,128)}, bf16[32,8192]{1,0:T(8,128)(2,1)}, bf16[32,8192]{1,0:T(8,128)(2,1)}) custom-call(f32[1,32]{1,0:T(1,128)} %get-tuple-element.12.share_in, f32[1,1]{1,0:T(1,128)} %get-tuple-element.13.sim_in, bf16[32,8192]{1,0:T(8,128)(2,1)} %get-tuple-element.14.early_in, ...), custom_call_target="tpu_custom_call" | custom-call | tf_op jit(solution)/shard_map/pallas_call | solution.py:585

commit v5 on v4

--- a/solution.py
+++ b/solution.py
@@ -15,7 +15,8 @@
 K_CORE = 1
 L_CORE = 0
 PIECES = 8
-ORDER = ((0, 0), (0, 1), (1, 0), (1, 1), (3, 0), (3, 1), (2, 0), (2, 1))
+ORDER = ((0, 0), (0, 1), (2, 0), (2, 1), (1, 0), (1, 1), (3, 0), (3, 1))
+OTHERS = tuple((dx, dy) for dx in (2, 1, 3, 0) for dy in (2, 1, 3, 0) if dx or dy)
 
 
 def send(src, dst, send_sem, recv_sem, gx, gy):
@@ -122,10 +123,15 @@
     load_y.start()
     barrier = pltpu.get_barrier_semaphore()
 
-    for r in range(1, 16):
-        other = lax.rem(chip + r, 16)
-        pl.semaphore_signal(barrier, inc=1, device_id=(2 * other, z), device_id_type=MESH)
-        pl.semaphore_signal(barrier, inc=1, device_id=(2 * other + 1, z), device_id_type=MESH)
+    for dx, dy in OTHERS:
+        other = chip_at(dx, dy)
+        pl.semaphore_signal(barrier, inc=1, device_id=(2 * other + core, z), device_id_type=MESH)
+
+    @pl.when(is_k)
+    def _():
+        for dx, dy in OTHERS:
+            other = chip_at(dx, dy)
+            pl.semaphore_signal(barrier, inc=1, device_id=(2 * other + L_CORE, z), device_id_type=MESH)
 
     for dz in (1, 2, 3):
         pl.semaphore_signal(barrier, inc=1, device_id=(2 * chip, level(dz)), device_id_type=MESH)
@@ -144,14 +150,14 @@
     load_y.wait()
 
     with jax.named_scope("barrier"):
-        pl.semaphore_wait(barrier, 37)
+        pl.semaphore_wait(barrier, 22 + 15 * (1 - core))
 
     def piece(j):
         dz, q = ORDER[j]
         return pl.ds(pl.multiple_of(32 * (4 * q + level(dz)), 32), 32)
 
     my_rows = pl.ds(pl.multiple_of(32 * (4 * core + z), 32), 32)
-    for dz in (1, 3, 2):
+    for dz in (2, 1, 3):
         to = level(dz)
         send(
             late.at[:, pl.ds(pl.multiple_of(2048 * to, 2048), 2048)],
@@ -163,9 +169,8 @@
         )
     own_cols = pl.ds(pl.multiple_of(2048 * z, 2048), 2048)
 
-    @pl.loop(1, 16)
-    def _(r):
-        other = lax.rem(chip + r, 16)
+    for dx, dy in OTHERS:
+        other = chip_at(dx, dy)
         send(cen.at[other], rt.at[gx], early_send, early_recv.at[x], 2 * other + K_CORE, z)
 
     def forward(src, dst, j, ex, ey):
@@ -181,7 +186,7 @@
     def _():
         send(late.at[:, own_cols], blocks.at[0, my_rows, :], pair_send.at[0], late_recv.at[1], l_dev, z)
         rt[gx] = cen[chip]
-        for dx in (0, 1, 3, 2):
+        for dx in (2, 1, 3, 0):
             xs = lax.rem(x + dx, 4)
             arrived(rt.at[0 : 8 if dx else 7], early_recv.at[xs], f"w_early{dx}")
 
@@ -492,16 +497,13 @@
         left(plane_sums.at[0:6], mean_send)
 
 
-CHUNKS = 4
-
-
 def publish(share_in, sim_in, early_in, late_in, share, sim, early, late, bufs, share_buf, sim_buf, in_sem, out_sem):
-    width = 8192 // CHUNKS
-    ways = [(share_in, share_buf, share), (sim_in, sim_buf, sim)]
-    for k, (src, dst) in enumerate(((early_in, early), (late_in, late))):
-        for c in range(CHUNKS):
-            at = pl.ds(width * c, width)
-            ways.append((src.at[:, at], bufs.at[CHUNKS * k + c], dst.at[:, at]))
+    ways = (
+        (early_in, bufs.at[0], early),
+        (late_in, bufs.at[1], late),
+        (share_in, share_buf, share),
+        (sim_in, sim_buf, sim),
+    )
     gets = [pltpu.make_async_copy(a, b, in_sem.at[n]) for n, (a, b, _) in enumerate(ways)]
     puts = [pltpu.make_async_copy(b, c, out_sem.at[n]) for n, (_, b, c) in enumerate(ways)]
     for get in gets:
@@ -593,11 +595,11 @@
         in_specs=[hbm] * 4,
         out_specs=(hbm,) * 4,
         scratch_shapes=[
-            vm((2 * CHUNKS, 32, 8192 // CHUNKS), BF16),
+            vm((2, 32, 8192), BF16),
             vm((1, 32), F32),
             vm((1, 1), F32),
-            dma((2 * CHUNKS + 2,)),
-            dma((2 * CHUNKS + 2,)),
+            dma((4,)),
+            dma((4,)),
         ],
     )(share, sim, early_rows, late_rows)
     return sim.reshape(()), share.reshape(32), early_rows, late_rows

time: 68.1 us -> 68.2 us (level)
  no operation moved by 1% of the time
where the time goes in v5:
time: 68.2 us; the launch traced here: 68 us
  Pallas kernels  67.4 us (99%)
    pallas_call x1, Pallas kernels, body(): pl.pallas_call(kernel, out_shape=(jax.ShapeDtypeStruct((1, 32), F32), jax...  64.7 us
    pallas_call x1, Pallas kernels, body(): pl.pallas_call(publish, out_shape=(jax.ShapeDtypeStruct((1, 32), F32), ja...  2.71 us

profile of v5, /device:TPU:1, one launch (start us, length us, event | category | flops | bytes accessed | tf_op | source)
XLA Modules:
  0.0 68.0 jit_solution(16880279931513553168)
XLA Ops:
  0.6 64.7 %shard_map.57 = (f32[1,32]{1,0:T(1,128)}, f32[1,1]{1,0:T(1,128)}, bf16[32,8192]{1,0:T(8,128)(2,1)}, bf16[32,8192]{1,0:T(8,128)(2,1)}) custom-call(bf16[64,4096]{1,0:T(8,128)(2,1)} %bitcast.3, bf16[32,8192]{1,0:T(8,128)(2,1)} %late_hbm.1), custom_call_target="tpu_custom_call" | custom-call | tf_op jit(solution)/shard_map/pallas_call | solution.py:523
  65.3 2.7 %shard_map.58 = (f32[1,32]{1,0:T(1,128)}, f32[1,1]{1,0:T(1,128)}, bf16[32,8192]{1,0:T(8,128)(2,1)}, bf16[32,8192]{1,0:T(8,128)(2,1)}) custom-call(f32[1,32]{1,0:T(1,128)} %get-tuple-element.12.share_in, f32[1,1]{1,0:T(1,128)} %get-tuple-element.13.sim_in, bf16[32,8192]{1,0:T(8,128)(2,1)} %get-tuple-element.14.early_in, ...), custom_call_target="tpu_custom_call" | custom-call | tf_op jit(solution)/shard_map/pallas_call | solution.py:587

commit v6 on v5

--- a/solution.py
+++ b/solution.py
@@ -16,6 +16,10 @@
 L_CORE = 0
 PIECES = 8
 ORDER = ((0, 0), (0, 1), (2, 0), (2, 1), (1, 0), (1, 1), (3, 0), (3, 1))
+EVERYONE = sorted(
+    [(dx, dy, dz) for dx in range(4) for dy in range(4) for dz in range(4)],
+    key=lambda d: -sum(min(v, 4 - v) for v in d),
+)
 OTHERS = tuple((dx, dy) for dx in (2, 1, 3, 0) for dy in (2, 1, 3, 0) if dx or dy)
 
 
@@ -61,8 +65,6 @@
     col_acc,
     msg,
     msg_in,
-    total,
-    total_in,
     load_sem,
     out_sem,
     late_send,
@@ -85,8 +87,6 @@
     part0_recv,
     msg_send,
     msg_recv,
-    total_send,
-    total_recv,
 ):
     gx = lax.axis_index("gx")
     z = lax.axis_index("gy")
@@ -433,29 +433,24 @@
                 else:
                     msg[r, :, 0:256] = jnp.zeros((1, 256), F32)
                 msg[r, :, 256:384] = scal
-        for dx in range(4):
-            for dy in range(4):
-                r = 4 * dx + dy
-                if r:
-                    send(msg.at[r], msg_in.at[r], msg_send, msg_recv, 2 * chip_at(dx, dy) + K_CORE, z)
+        for dx, dy, dz in EVERYONE:
+            r = 4 * dx + dy
+            there = msg_in.at[16 * dz + r]
+            chip_there = 2 * chip_at(dx, dy)
+            if dx or dy or dz:
+                send(msg.at[r], there, msg_send.at[K_CORE], msg_recv, chip_there + K_CORE, level(dz))
+            send(msg.at[r], there, msg_send.at[L_CORE], msg_recv, chip_there + L_CORE, level(dz))
         msg_in[0] = msg[0]
-        arrived(msg_in.at[0:15], msg_recv, "w_msg")
-        s = msg_in[0]
-        for r in range(1, 16):
-            s = s + msg_in[r]
-        total[...] = s
-        for dz in (1, 2, 3):
-            send(total, total_in.at[dz - 1], total_send, total_recv, k_dev, level(dz))
-            send(total, total_in.at[dz - 1], total_send, total_recv, l_dev, level(dz))
-        send(total, total_in.at[3], pair_send.at[2], total_recv, l_dev, z)
-        total_in[3] = total[...]
-        arrived(total_in.at[0:3], total_recv, "w_tot")
+        arrived(msg_in.at[0:63], msg_recv, "w_msg")
 
     @pl.when(is_l)
     def _():
-        arrived(total_in, total_recv, "w_tot")
-
-    final = (total_in[0] + total_in[1]) + (total_in[2] + total_in[3])
+        arrived(msg_in, msg_recv, "w_msg")
+
+    rows = [msg_in[r] for r in range(64)]
+    while len(rows) > 1:
+        rows = [a + b for a, b in zip(rows[0::2], rows[1::2])]
+    final = rows[0]
     scal_lane = lax.broadcasted_iota(jnp.int32, (1, 128), 1)
     scal = final[:, 256:384]
     kk, ll, kl = (jnp.sum(jnp.where(scal_lane == j, scal, 0.0), axis=1, keepdims=True) for j in range(3))
@@ -481,10 +476,9 @@
     def _():
         left(late.at[:, 0:2048], pair_send.at[0])
         left(early_pieces.at[0], pair_send.at[1])
-        left(total, pair_send.at[2])
         left(blocks.at[0, 0:192, :], rows_send)
-        left(msg.at[0:15], msg_send)
-        left(msg.at[0:6], total_send)
+        left(msg_in.at[0:63], msg_send.at[K_CORE])
+        left(msg_in, msg_send.at[L_CORE])
 
     @pl.when(is_l)
     def _():
@@ -554,9 +548,7 @@
             vm((32, 128), F32),
             vm((8, 256), F32),
             vm((16, 1, 384), F32),
-            vm((16, 1, 384), F32),
-            vm((1, 384), F32),
-            vm((4, 1, 384), F32),
+            vm((64, 1, 384), F32),
             dma((2,)),
             dma((2,)),
             dma,
@@ -577,9 +569,7 @@
             dma,
             dma,
             dma,
-            dma,
-            dma,
-            dma,
+            dma((2,)),
             dma,
         ],
         compiler_params=pltpu.CompilerParams(collective_id=0, has_side_effects=True, vmem_limit_bytes=67043328),

time: 68.2 us -> 67.3 us (0.987)
  Pallas kernels: 67.4 us -> 66.5 us
    pallas_call x1, Pallas kernels: 64.7 us -> 63.8 us  [body(): pl.pallas_call(kernel, out_shape=(jax.ShapeDtypeStruct((1, 32), F32), jax...]
where the time goes in v6:
time: 67.3 us; the launch traced here: 67.1 us
  Pallas kernels  66.5 us (99%)
    pallas_call x1, Pallas kernels, body(): pl.pallas_call(kernel, out_shape=(jax.ShapeDtypeStruct((1, 32), F32), jax...  63.8 us
    pallas_call x1, Pallas kernels, body(): pl.pallas_call(publish, out_shape=(jax.ShapeDtypeStruct((1, 32), F32), ja...  2.71 us

profile of v6, /device:TPU:1, one launch (start us, length us, event | category | flops | bytes accessed | tf_op | source)
XLA Modules:
  0.0 67.1 jit_solution(5820010425906059597)
XLA Ops:
  0.6 63.8 %shard_map.57 = (f32[1,32]{1,0:T(1,128)}, f32[1,1]{1,0:T(1,128)}, bf16[32,8192]{1,0:T(8,128)(2,1)}, bf16[32,8192]{1,0:T(8,128)(2,1)}) custom-call(bf16[64,4096]{1,0:T(8,128)(2,1)} %bitcast.3, bf16[32,8192]{1,0:T(8,128)(2,1)} %late_hbm.1), custom_call_target="tpu_custom_call" | custom-call | tf_op jit(solution)/shard_map/pallas_call | solution.py:517
  64.4 2.7 %shard_map.58 = (f32[1,32]{1,0:T(1,128)}, f32[1,1]{1,0:T(1,128)}, bf16[32,8192]{1,0:T(8,128)(2,1)}, bf16[32,8192]{1,0:T(8,128)(2,1)}) custom-call(f32[1,32]{1,0:T(1,128)} %get-tuple-element.12.share_in, f32[1,1]{1,0:T(1,128)} %get-tuple-element.13.sim_in, bf16[32,8192]{1,0:T(8,128)(2,1)} %get-tuple-element.14.early_in, ...), custom_call_target="tpu_custom_call" | custom-call | tf_op jit(solution)/shard_map/pallas_call | solution.py:577

commit v7 on v6

--- a/solution.py
+++ b/solution.py
@@ -15,6 +15,7 @@
 K_CORE = 1
 L_CORE = 0
 PIECES = 8
+DETOUR = (2, 3)
 ORDER = ((0, 0), (0, 1), (2, 0), (2, 1), (1, 0), (1, 1), (3, 0), (3, 1))
 EVERYONE = sorted(
     [(dx, dy, dz) for dx in range(4) for dy in range(4) for dz in range(4)],
@@ -178,9 +179,8 @@
         rows = piece(j)
         send(blocks.at[src, rows, :], blocks.at[dst, rows, :], gather_send, gather_recv.at[dst - 1, j], to, z)
 
-    def start(j):
-        forward(0, 1, j, 1, 0)
-        forward(0, 2, j, 0, 1)
+    def take(slot, j):
+        arrived(blocks.at[slot, piece(j), :], gather_recv.at[slot - 1, j], f"g{slot}_{j}")
 
     @pl.when(is_k)
     def _():
@@ -198,7 +198,8 @@
                 blocks[0, :, at] = cols.T.astype(BF16)
 
         for j in range(PIECES):
-            start(j)
+            forward(0, 1, j, 1, 0)
+            forward(0, 2, j, 0, 1)
         for dz in (1, 2, 3):
             for q in (0, 1):
                 rows = pl.ds(pl.multiple_of(32 * (4 * q + level(dz)), 32), 32)
@@ -206,6 +207,11 @@
         rows = pl.ds(pl.multiple_of(32 * (4 * L_CORE + z), 32), 32)
         send(blocks.at[0, rows, :], early_pieces.at[z], pair_send.at[1], rows_recv, l_dev, z)
         early_pieces[z] = blocks[0, my_rows, :]
+
+    def start(j):
+        forward(0, 2, j, 0, 1)
+        if j not in DETOUR:
+            forward(0, 1, j, 1, 0)
 
     @pl.when(is_l)
     def _():
@@ -331,23 +337,50 @@
         row_cols[...] = jnp.zeros_like(row_cols)
         half_cols[...] = jnp.zeros_like(half_cols)
         col_acc[...] = jnp.zeros_like(col_acc)
-
         product(0)
-
-    for j in range(PIECES):
-        rows = piece(j)
-        arrived(blocks.at[1, rows, :], gather_recv.at[0, j], f"w1_{j}")
-        forward(1, 4, j, 0, 3)
-        arrived(blocks.at[2, rows, :], gather_recv.at[1, j], f"w2_{j}")
-        forward(2, 5, j, 3, 0)
-        pl.when(is_k)(lambda: forward(1, 3, j, 0, 1))
-        if j == 6:
-            pl.when(is_l)(late_mean)
+        for j in range(PIECES):
+            take(1, j)
+            forward(1, 4, j, 0, 3)
+            if j % 2 == 0:
+                forward(1, 3, j, 0, 1)
+            take(2, j)
+            forward(2, 5, j, 3, 0)
+            if j % 2:
+                forward(2, 3, j, 1, 0)
 
     @pl.when(is_l)
     def _():
+        def from_1(j):
+            take(1, j)
+            forward(1, 4, j, 0, 3)
+
+        def from_2(j):
+            take(2, j)
+            forward(2, 5, j, 3, 0)
+            if j in DETOUR:
+                forward(2, 3, j, 1, 0)
+
+        def from_3(j):
+            take(3, j)
+            forward(3, 1, j, 0, 3)
+
+        for near, far in ((0, 0), (1, 1), (4, 2), (5, 3), (6, 4), (7, 5)):
+            from_1(near)
+            from_2(far)
+        from_3(DETOUR[0])
+        from_2(6)
+        late_mean()
+        from_3(DETOUR[1])
+        from_2(7)
         for j in range(PIECES):
-            forward(2, 3, j, 1, 0)
+            if j in DETOUR:
+                continue
+            if j in (4, 5, 6):
+                forward(2, 3, j, 1, 0)
+            else:
+                forward(1, 3, j, 0, 1)
+        for j in DETOUR:
+            from_1(j)
 
     @pl.when(is_l)
     def _():
@@ -384,15 +417,11 @@
     put_e.start()
     put_l.start()
 
-    def take(slot):
+    for slot in (4, 5):
         for j in range(PIECES):
-            arrived(blocks.at[slot, piece(j), :], gather_recv.at[slot - 1, j], f"w{slot}_{j}")
+            take(slot, j)
         pl.when(is_l)(lambda: center(slot))
-
-    take(4)
-    product(4)
-    take(5)
-    product(5)
+        product(slot)
     product(7)
 
     @pl.when(is_k)
@@ -400,7 +429,12 @@
         for t in (0, 1, 2, 3):
             settle(t)
 
-    take(3)
+    for j in range(PIECES):
+        if j in DETOUR:
+            pl.when(is_k)(lambda: take(3, j))
+        else:
+            take(3, j)
+    pl.when(is_l)(lambda: center(3))
     for t in (6, 8, 9):
         product(t)
 

time: 67.3 us -> 66.1 us (0.982)
  Pallas kernels: 66.5 us -> 65.2 us
    pallas_call x1, Pallas kernels: 63.8 us -> 62.5 us  [body(): pl.pallas_call(kernel, out_shape=(jax.ShapeDtypeStruct((1, 32), F32), jax...]
where the time goes in v7:
time: 66.1 us; the launch traced here: 65.9 us
  Pallas kernels  65.2 us (99%)
    pallas_call x1, Pallas kernels, body(): pl.pallas_call(kernel, out_shape=(jax.ShapeDtypeStruct((1, 32), F32), jax...  62.5 us
    pallas_call x1, Pallas kernels, body(): pl.pallas_call(publish, out_shape=(jax.ShapeDtypeStruct((1, 32), F32), ja...  2.71 us

profile of v7, /device:TPU:1, one launch (start us, length us, event | category | flops | bytes accessed | tf_op | source)
XLA Modules:
  0.0 65.9 jit_solution(3909643653896212936)
XLA Ops:
  0.6 62.5 %shard_map.57 = (f32[1,32]{1,0:T(1,128)}, f32[1,1]{1,0:T(1,128)}, bf16[32,8192]{1,0:T(8,128)(2,1)}, bf16[32,8192]{1,0:T(8,128)(2,1)}) custom-call(bf16[64,4096]{1,0:T(8,128)(2,1)} %bitcast.3, bf16[32,8192]{1,0:T(8,128)(2,1)} %late_hbm.1), custom_call_target="tpu_custom_call" | custom-call | tf_op jit(solution)/shard_map/pallas_call | solution.py:551
  63.2 2.7 %shard_map.58 = (f32[1,32]{1,0:T(1,128)}, f32[1,1]{1,0:T(1,128)}, bf16[32,8192]{1,0:T(8,128)(2,1)}, bf16[32,8192]{1,0:T(8,128)(2,1)}) custom-call(f32[1,32]{1,0:T(1,128)} %get-tuple-element.12.share_in, f32[1,1]{1,0:T(1,128)} %get-tuple-element.13.sim_in, bf16[32,8192]{1,0:T(8,128)(2,1)} %get-tuple-element.14.early_in, ...), custom_call_target="tpu_custom_call" | custom-call | tf_op jit(solution)/shard_map/pallas_call | solution.py:611

commit v8 on v7

--- a/solution.py
+++ b/solution.py
@@ -209,8 +209,9 @@
         early_pieces[z] = blocks[0, my_rows, :]
 
     def start(j):
-        forward(0, 2, j, 0, 1)
-        if j not in DETOUR:
+        if j != DETOUR[1]:
+            forward(0, 2, j, 0, 1)
+        if j != DETOUR[0]:
             forward(0, 1, j, 1, 0)
 
     @pl.when(is_l)
@@ -353,34 +354,29 @@
         def from_1(j):
             take(1, j)
             forward(1, 4, j, 0, 3)
+            if j == DETOUR[1]:
+                forward(1, 3, j, 0, 1)
 
         def from_2(j):
             take(2, j)
             forward(2, 5, j, 3, 0)
-            if j in DETOUR:
+            if j == DETOUR[0]:
                 forward(2, 3, j, 1, 0)
 
-        def from_3(j):
-            take(3, j)
-            forward(3, 1, j, 0, 3)
-
-        for near, far in ((0, 0), (1, 1), (4, 2), (5, 3), (6, 4), (7, 5)):
+        for near, far in ((0, 0), (1, 1), (3, 2), (4, 4), (5, 5), (6, 6), (7, 7)):
             from_1(near)
             from_2(far)
-        from_3(DETOUR[0])
-        from_2(6)
+        for j in (0, 1, 4):
+            forward(1, 3, j, 0, 1)
+        for j in (5, 6, 7):
+            forward(2, 3, j, 1, 0)
+        take(3, DETOUR[0])
+        forward(3, 1, DETOUR[0], 0, 3)
+        take(3, DETOUR[1])
+        forward(3, 2, DETOUR[1], 3, 0)
         late_mean()
-        from_3(DETOUR[1])
-        from_2(7)
-        for j in range(PIECES):
-            if j in DETOUR:
-                continue
-            if j in (4, 5, 6):
-                forward(2, 3, j, 1, 0)
-            else:
-                forward(1, 3, j, 0, 1)
-        for j in DETOUR:
-            from_1(j)
+        from_2(DETOUR[1])
+        from_1(DETOUR[0])
 
     @pl.when(is_l)
     def _():

time: 66.1 us -> 66.2 us (level)
  no operation moved by 1% of the time
where the time goes in v8:
time: 66.2 us; the launch traced here: 66 us
  Pallas kernels  65.4 us (99%)
    pallas_call x1, Pallas kernels, body(): pl.pallas_call(kernel, out_shape=(jax.ShapeDtypeStruct((1, 32), F32), jax...  62.7 us
    pallas_call x1, Pallas kernels, body(): pl.pallas_call(publish, out_shape=(jax.ShapeDtypeStruct((1, 32), F32), ja...  2.71 us

profile of v8, /device:TPU:1, one launch (start us, length us, event | category | flops | bytes accessed | tf_op | source)
XLA Modules:
  0.0 66.0 jit_solution(14603830404529194164)
XLA Ops:
  0.6 62.7 %shard_map.57 = (f32[1,32]{1,0:T(1,128)}, f32[1,1]{1,0:T(1,128)}, bf16[32,8192]{1,0:T(8,128)(2,1)}, bf16[32,8192]{1,0:T(8,128)(2,1)}) custom-call(bf16[64,4096]{1,0:T(8,128)(2,1)} %bitcast.3, bf16[32,8192]{1,0:T(8,128)(2,1)} %late_hbm.1), custom_call_target="tpu_custom_call" | custom-call | tf_op jit(solution)/shard_map/pallas_call | solution.py:547
  63.3 2.7 %shard_map.58 = (f32[1,32]{1,0:T(1,128)}, f32[1,1]{1,0:T(1,128)}, bf16[32,8192]{1,0:T(8,128)(2,1)}, bf16[32,8192]{1,0:T(8,128)(2,1)}) custom-call(f32[1,32]{1,0:T(1,128)} %get-tuple-element.12.share_in, f32[1,1]{1,0:T(1,128)} %get-tuple-element.13.sim_in, bf16[32,8192]{1,0:T(8,128)(2,1)} %get-tuple-element.14.early_in, ...), custom_call_target="tpu_custom_call" | custom-call | tf_op jit(solution)/shard_map/pallas_call | solution.py:607

commit v9 on v8

--- a/solution.py
+++ b/solution.py
@@ -370,11 +370,11 @@
             forward(1, 3, j, 0, 1)
         for j in (5, 6, 7):
             forward(2, 3, j, 1, 0)
+        late_mean()
         take(3, DETOUR[0])
         forward(3, 1, DETOUR[0], 0, 3)
         take(3, DETOUR[1])
         forward(3, 2, DETOUR[1], 3, 0)
-        late_mean()
         from_2(DETOUR[1])
         from_1(DETOUR[0])
 
@@ -420,11 +420,6 @@
         product(slot)
     product(7)
 
-    @pl.when(is_k)
-    def _():
-        for t in (0, 1, 2, 3):
-            settle(t)
-
     for j in range(PIECES):
         if j in DETOUR:
             pl.when(is_k)(lambda: take(3, j))
@@ -436,7 +431,7 @@
 
     @pl.when(is_k)
     def _():
-        for t in (4, 5, 7, 6, 8, 9):
+        for t in (0, 1, 2, 3, 4, 5, 7, 6, 8, 9):
             settle(t)
         turned = jnp.concatenate([row_cols[...]] * 4, axis=0).T
         half_turned = jnp.concatenate([half_cols[...]] * 8, axis=0).T

time: 66.2 us -> 66.2 us (level)
  no operation moved by 1% of the time
where the time goes in v9:
time: 66.2 us; the launch traced here: 66 us
  Pallas kernels  65.4 us (99%)
    pallas_call x1, Pallas kernels, body(): pl.pallas_call(kernel, out_shape=(jax.ShapeDtypeStruct((1, 32), F32), jax...  62.7 us
    pallas_call x1, Pallas kernels, body(): pl.pallas_call(publish, out_shape=(jax.ShapeDtypeStruct((1, 32), F32), ja...  2.71 us

profile of v9, /device:TPU:1, one launch (start us, length us, event | category | flops | bytes accessed | tf_op | source)
XLA Modules:
  0.0 66.0 jit_solution(3040825738594626625)
XLA Ops:
  0.6 62.7 %shard_map.57 = (f32[1,32]{1,0:T(1,128)}, f32[1,1]{1,0:T(1,128)}, bf16[32,8192]{1,0:T(8,128)(2,1)}, bf16[32,8192]{1,0:T(8,128)(2,1)}) custom-call(bf16[64,4096]{1,0:T(8,128)(2,1)} %bitcast.3, bf16[32,8192]{1,0:T(8,128)(2,1)} %late_hbm.1), custom_call_target="tpu_custom_call" | custom-call | tf_op jit(solution)/shard_map/pallas_call | solution.py:542
  63.3 2.7 %shard_map.58 = (f32[1,32]{1,0:T(1,128)}, f32[1,1]{1,0:T(1,128)}, bf16[32,8192]{1,0:T(8,128)(2,1)}, bf16[32,8192]{1,0:T(8,128)(2,1)}) custom-call(f32[1,32]{1,0:T(1,128)} %get-tuple-element.12.share_in, f32[1,1]{1,0:T(1,128)} %get-tuple-element.13.sim_in, bf16[32,8192]{1,0:T(8,128)(2,1)} %get-tuple-element.14.early_in, ...), custom_call_target="tpu_custom_call" | custom-call | tf_op jit(solution)/shard_map/pallas_call | solution.py:602

commit v10 on v9

--- a/solution.py
+++ b/solution.py
@@ -10,13 +10,27 @@
 BF16 = jnp.bfloat16
 
 SLOTS = ((0, 0), (1, 0), (0, 1), (1, 1), (1, 3), (3, 1))
-TILES = ((0, 0), (1, 0), (2, 0), (1, 2), (4, 2), (5, 1), (3, 0), (4, 5), (3, 5), (3, 4))
-SHARED = 7
+TILES = (
+    (0, 0, None),
+    (1, 2, None),
+    (4, 2, None),
+    (5, 1, None),
+    (1, 0, 0),
+    (1, 0, 1),
+    (2, 0, 0),
+    (2, 0, 1),
+    (3, 0, 0),
+    (3, 0, 1),
+    (4, 5, "x"),
+    (3, 5, "x"),
+    (3, 4, "y"),
+)
+WHOLE = 4
 K_CORE = 1
 L_CORE = 0
 PIECES = 8
-DETOUR = (2, 3)
-ORDER = ((0, 0), (0, 1), (2, 0), (2, 1), (1, 0), (1, 1), (3, 0), (3, 1))
+DETOUR = (5, 6)
+ORDER = ((0, 0), (2, 0), (1, 0), (3, 0), (0, 1), (2, 1), (1, 1), (3, 1))
 EVERYONE = sorted(
     [(dx, dy, dz) for dx in range(4) for dy in range(4) for dz in range(4)],
     key=lambda d: -sum(min(v, 4 - v) for v in d),
@@ -218,10 +232,10 @@
     def _():
         send(cen.at[chip], rt.at[gx], pair_send.at[0], early_recv.at[x], k_dev, z)
         blocks[0, my_rows, :] = late[:, own_cols]
-        for j in range(PIECES):
+        for n, j in enumerate((0, 4, 1, 5, 2, 6, 3, 7)):
             if j:
                 arrived(blocks.at[0, piece(j), :], late_recv.at[2 * ORDER[j][0] + ORDER[j][1]], f"w_late{j}")
-            if j < 6:
+            if n < 6:
                 start(j)
         for c in range(4):
             at = slice(512 * c, 512 * (c + 1))
@@ -236,14 +250,14 @@
             other = lax.rem(chip + r, 16)
             send(own_sum, plane_sums.at[chip], sums_send, sums_recv, 2 * other + L_CORE, z)
 
-        start(6)
+        start(3)
         start(7)
 
-    def center(slot):
+    def center(slot, half=None):
         for c in range(4):
             at = slice(512 * c, 512 * (c + 1))
             m = mean_out[:, at]
-            for r in range(8):
+            for r in range(8) if half is None else range(4 * half, 4 * half + 4):
                 rows = slice(32 * r, 32 * (r + 1))
                 blocks[6 + slot, rows, at] = (blocks[slot, rows, at].astype(F32) - m).astype(BF16)
 
@@ -266,16 +280,16 @@
     ready = 6 * (1 - core)
 
     def sides(t):
-        a, b = TILES[t]
-        if t < SHARED:
-            return a, b, 0
-        half = (y if t == 9 else x) // 2
-        return a + half * (b - a), b + half * (a - b), half
+        a, b, half = TILES[t]
+        if half in ("x", "y"):
+            half = (x if half == "x" else y) // 2
+            return a + half * (b - a), b + half * (a - b), half
+        return a, b, half
 
     def product(t):
         a, b, half = sides(t)
         with jax.named_scope(f"dot{t}"):
-            if t < SHARED:
+            if t < WHOLE:
                 gram[t] = lax.dot_general(blocks[a + ready], blocks[b + ready], dims, preferred_element_type=F32)
             else:
                 top = pl.ds(pl.multiple_of(128 * half, 128), 128)
@@ -284,11 +298,11 @@
                 )
         if t == 0:
             src, dst, size, out, into, pair = gram.at[0], parts0, 64, part0_send, part0_recv, 2
-        elif t < SHARED:
+        elif t < WHOLE:
             src, dst, size, out, into, pair = stage.at[t - 1], parts.at[t - 1], 64, part_send, part_recv.at[t - 1], 3
             stage[t - 1] = gram[t].astype(BF16)
         else:
-            n = t - SHARED
+            n = t - WHOLE
             src, dst, size, out, into, pair = halves.at[n], half_parts.at[n], 32, half_send, part_recv.at[t - 1], 4
             halves[n] = gram[t, 0:128, :].astype(BF16)
         for dz in (1, 2, 3):
@@ -305,10 +319,10 @@
         _, b, _ = sides(t)
         if t == 0:
             size, buf, sem = 64, parts0, part0_recv
-        elif t < SHARED:
+        elif t < WHOLE:
             size, buf, sem = 64, parts.at[t - 1], part_recv.at[t - 1]
         else:
-            size, buf, sem = 32, half_parts.at[t - SHARED], part_recv.at[t - 1]
+            size, buf, sem = 32, half_parts.at[t - WHOLE], part_recv.at[t - 1]
         arrived(buf, sem, f"wp{t}")
         part = [buf[n].astype(F32) for n in range(7)]
         rows = pl.ds(pl.multiple_of(size * z, size), size)
@@ -322,7 +336,7 @@
             weight = 2.0
             across = jnp.sum(h, axis=0, keepdims=True)
             col_acc[...] += jnp.where(slot_row == b, across, 0.0)
-        if t < SHARED:
+        if t < WHOLE:
             row_cols[...] += own
         else:
             half_cols[...] += own
@@ -348,6 +362,9 @@
             forward(2, 5, j, 3, 0)
             if j % 2:
                 forward(2, 3, j, 1, 0)
+            if j == 3:
+                product(4)
+                product(6)
 
     @pl.when(is_l)
     def _():
@@ -363,27 +380,29 @@
             if j == DETOUR[0]:
                 forward(2, 3, j, 1, 0)
 
-        for near, far in ((0, 0), (1, 1), (3, 2), (4, 4), (5, 5), (6, 6), (7, 7)):
+        for near, far in ((0, 0), (4, 4), (1, 1), (2, 5), (6, 2), (3, 3), (7, 7)):
             from_1(near)
             from_2(far)
-        for j in (0, 1, 4):
-            forward(1, 3, j, 0, 1)
-        for j in (5, 6, 7):
-            forward(2, 3, j, 1, 0)
         late_mean()
+        center(1, 0)
+        product(4)
+        center(2, 0)
+        product(6)
+        for j in (0, 1, 2, 3, 4, 7):
+            if j % 2:
+                forward(1, 3, j, 0, 1)
+            else:
+                forward(2, 3, j, 1, 0)
         take(3, DETOUR[0])
         forward(3, 1, DETOUR[0], 0, 3)
         take(3, DETOUR[1])
         forward(3, 2, DETOUR[1], 3, 0)
         from_2(DETOUR[1])
         from_1(DETOUR[0])
-
-    @pl.when(is_l)
-    def _():
-        center(1)
-        center(2)
-
-    for t in (1, 2, 3):
+        center(1, 1)
+        center(2, 1)
+
+    for t in (5, 7, 1):
         product(t)
 
     @pl.when(is_k)
@@ -413,25 +432,28 @@
     put_e.start()
     put_l.start()
 
-    for slot in (4, 5):
+    for j in range(4):
+        take(3, j)
+    pl.when(is_l)(lambda: center(3, 0))
+    product(8)
+    for slot, t in ((4, 2), (5, 3)):
         for j in range(PIECES):
             take(slot, j)
         pl.when(is_l)(lambda: center(slot))
-        product(slot)
-    product(7)
-
-    for j in range(PIECES):
+        product(t)
+    product(10)
+    for j in range(4, PIECES):
         if j in DETOUR:
             pl.when(is_k)(lambda: take(3, j))
         else:
             take(3, j)
-    pl.when(is_l)(lambda: center(3))
-    for t in (6, 8, 9):
+    pl.when(is_l)(lambda: center(3, 1))
+    for t in (9, 11, 12):
         product(t)
 
     @pl.when(is_k)
     def _():
-        for t in (0, 1, 2, 3, 4, 5, 7, 6, 8, 9):
+        for t in (0, 4, 6, 5, 7, 1, 8, 2, 3, 10, 9, 11, 12):
             settle(t)
         turned = jnp.concatenate([row_cols[...]] * 4, axis=0).T
         half_turned = jnp.concatenate([half_cols[...]] * 8, axis=0).T
@@ -439,7 +461,7 @@
         both = col_acc[...]
         for t in range(len(TILES)):
             a, _, half = sides(t)
-            if t < SHARED:
+            if t < WHOLE:
                 row = jnp.where(col // 64 == z, turned[t : t + 1, :], 0.0)
             else:
                 row = jnp.where(col // 32 == 4 * half + z, half_turned[t : t + 1, :], 0.0)
@@ -555,11 +577,11 @@
             vm((16, 64, 256), BF16),
             vm((32, 64, 256), BF16),
             vm((12, 256, 2048), BF16),
-            vm((10, 256, 256), F32),
-            vm((6, 256, 256), BF16),
-            vm((6, 7, 64, 256), BF16),
-            vm((3, 128, 256), BF16),
-            vm((3, 7, 32, 256), BF16),
+            vm((13, 256, 256), F32),
+            vm((3, 256, 256), BF16),
+            vm((3, 7, 64, 256), BF16),
+            vm((9, 128, 256), BF16),
+            vm((9, 7, 32, 256), BF16),
             vm((7, 64, 256), F32),
             vm((1, 2048), F32),
             vm((16, 1, 2048), F32),
@@ -590,7 +612,7 @@
             dma,
             dma,
             dma,
-            dma((9,)),
+            dma((12,)),
             dma,
             dma,
             dma,

time: 66.2 us -> 65.5 us (0.989)
  Pallas kernels: 65.4 us -> 64.7 us
    pallas_call x1, Pallas kernels: 62.7 us -> 62 us  [body(): pl.pallas_call(kernel, out_shape=(jax.ShapeDtypeStruct((1, 32), F32), jax...]
where the time goes in v10:
time: 65.5 us; the launch traced here: 65.3 us
  Pallas kernels  64.7 us (99%)
    pallas_call x1, Pallas kernels, body(): pl.pallas_call(kernel, out_shape=(jax.ShapeDtypeStruct((1, 32), F32), jax...  62 us
    pallas_call x1, Pallas kernels, body(): pl.pallas_call(publish, out_shape=(jax.ShapeDtypeStruct((1, 32), F32), ja...  2.71 us

profile of v10, /device:TPU:1, one launch (start us, length us, event | category | flops | bytes accessed | tf_op | source)
XLA Modules:
  0.0 65.3 jit_solution(15327309464352549491)
XLA Ops:
  0.6 62.0 %shard_map.57 = (f32[1,32]{1,0:T(1,128)}, f32[1,1]{1,0:T(1,128)}, bf16[32,8192]{1,0:T(8,128)(2,1)}, bf16[32,8192]{1,0:T(8,128)(2,1)}) custom-call(bf16[64,4096]{1,0:T(8,128)(2,1)} %bitcast.3, bf16[32,8192]{1,0:T(8,128)(2,1)} %late_hbm.1), custom_call_target="tpu_custom_call" | custom-call | tf_op jit(solution)/shard_map/pallas_call | solution.py:564
  62.6 2.7 %shard_map.58 = (f32[1,32]{1,0:T(1,128)}, f32[1,1]{1,0:T(1,128)}, bf16[32,8192]{1,0:T(8,128)(2,1)}, bf16[32,8192]{1,0:T(8,128)(2,1)}) custom-call(f32[1,32]{1,0:T(1,128)} %get-tuple-element.12.share_in, f32[1,1]{1,0:T(1,128)} %get-tuple-element.13.sim_in, bf16[32,8192]{1,0:T(8,128)(2,1)} %get-tuple-element.14.early_in, ...), custom_call_target="tpu_custom_call" | custom-call | tf_op jit(solution)/shard_map/pallas_call | solution.py:624

commit v11 on v10

--- a/solution.py
+++ b/solution.py
@@ -305,7 +305,7 @@
             n = t - WHOLE
             src, dst, size, out, into, pair = halves.at[n], half_parts.at[n], 32, half_send, part_recv.at[t - 1], 4
             halves[n] = gram[t, 0:128, :].astype(BF16)
-        for dz in (1, 2, 3):
+        for dz in (2, 1, 3):
             to = level(dz)
             rows = pl.ds(pl.multiple_of(size * to, size), size)
             send(src.at[rows, :], dst.at[dz - 1 + 4 * (1 - core)], out, into, k_dev, to)
@@ -453,10 +453,14 @@
 
     @pl.when(is_k)
     def _():
-        for t in (0, 4, 6, 5, 7, 1, 8, 2, 3, 10, 9, 11, 12):
+        for t in (0, 4, 6, 5, 7, 1, 8, 2, 3):
             settle(t)
-        turned = jnp.concatenate([row_cols[...]] * 4, axis=0).T
-        half_turned = jnp.concatenate([half_cols[...]] * 8, axis=0).T
+        turned = jnp.concatenate([row_cols[...]] * 2, axis=0).T
+        turned = jnp.concatenate([turned] * 2, axis=1)
+        for t in (10, 9, 11, 12):
+            settle(t)
+        half_turned = jnp.concatenate([half_cols[...]] * 4, axis=0).T
+        half_turned = jnp.concatenate([half_turned] * 2, axis=1)
         col = lax.broadcasted_iota(jnp.int32, (1, 256), 1)
         both = col_acc[...]
         for t in range(len(TILES)):

time: 65.5 us -> 65.6 us (level)
  no operation moved by 1% of the time
where the time goes in v11:
time: 65.6 us; the launch traced here: 65.4 us
  Pallas kernels  64.8 us (99%)
    pallas_call x1, Pallas kernels, body(): pl.pallas_call(kernel, out_shape=(jax.ShapeDtypeStruct((1, 32), F32), jax...  62.1 us
    pallas_call x1, Pallas kernels, body(): pl.pallas_call(publish, out_shape=(jax.ShapeDtypeStruct((1, 32), F32), ja...  2.71 us

profile of v11, /device:TPU:1, one launch (start us, length us, event | category | flops | bytes accessed | tf_op | source)
XLA Modules:
  0.0 65.4 jit_solution(13313026998732826571)
XLA Ops:
  0.6 62.1 %shard_map.57 = (f32[1,32]{1,0:T(1,128)}, f32[1,1]{1,0:T(1,128)}, bf16[32,8192]{1,0:T(8,128)(2,1)}, bf16[32,8192]{1,0:T(8,128)(2,1)}) custom-call(bf16[64,4096]{1,0:T(8,128)(2,1)} %bitcast.3, bf16[32,8192]{1,0:T(8,128)(2,1)} %late_hbm.1), custom_call_target="tpu_custom_call" | custom-call | tf_op jit(solution)/shard_map/pallas_call | solution.py:568
  62.7 2.7 %shard_map.58 = (f32[1,32]{1,0:T(1,128)}, f32[1,1]{1,0:T(1,128)}, bf16[32,8192]{1,0:T(8,128)(2,1)}, bf16[32,8192]{1,0:T(8,128)(2,1)}) custom-call(f32[1,32]{1,0:T(1,128)} %get-tuple-element.12.share_in, f32[1,1]{1,0:T(1,128)} %get-tuple-element.13.sim_in, bf16[32,8192]{1,0:T(8,128)(2,1)} %get-tuple-element.14.early_in, ...), custom_call_target="tpu_custom_call" | custom-call | tf_op jit(solution)/shard_map/pallas_call | solution.py:628

commit v12 on v11

--- a/solution.py
+++ b/solution.py
@@ -76,7 +76,6 @@
     late_out,
     acc,
     row_cols,
-    half_cols,
     col_acc,
     msg,
     msg_in,
@@ -293,56 +292,58 @@
                 gram[t] = lax.dot_general(blocks[a + ready], blocks[b + ready], dims, preferred_element_type=F32)
             else:
                 top = pl.ds(pl.multiple_of(128 * half, 128), 128)
-                gram[t, 0:128, :] = lax.dot_general(
-                    blocks[a + ready, top, :], blocks[b + ready], dims, preferred_element_type=F32
+                gram[t, :, 0:128] = lax.dot_general(
+                    blocks[b + ready], blocks[a + ready, top, :], dims, preferred_element_type=F32
                 )
         if t == 0:
-            src, dst, size, out, into, pair = gram.at[0], parts0, 64, part0_send, part0_recv, 2
+            src, dst, out, into, pair = gram.at[0], parts0, part0_send, part0_recv, 2
         elif t < WHOLE:
-            src, dst, size, out, into, pair = stage.at[t - 1], parts.at[t - 1], 64, part_send, part_recv.at[t - 1], 3
+            src, dst, out, into, pair = stage.at[t - 1], parts.at[t - 1], part_send, part_recv.at[t - 1], 3
             stage[t - 1] = gram[t].astype(BF16)
         else:
             n = t - WHOLE
-            src, dst, size, out, into, pair = halves.at[n], half_parts.at[n], 32, half_send, part_recv.at[t - 1], 4
-            halves[n] = gram[t, 0:128, :].astype(BF16)
+            src, dst, out, into, pair = halves.at[n], half_parts.at[n], half_send, part_recv.at[t - 1], 4
+            halves[n] = gram[t, :, 0:128].astype(BF16)
         for dz in (2, 1, 3):
             to = level(dz)
-            rows = pl.ds(pl.multiple_of(size * to, size), size)
+            rows = pl.ds(pl.multiple_of(64 * to, 64), 64)
             send(src.at[rows, :], dst.at[dz - 1 + 4 * (1 - core)], out, into, k_dev, to)
 
         @pl.when(is_l)
         def _():
-            rows = pl.ds(pl.multiple_of(size * z, size), size)
+            rows = pl.ds(pl.multiple_of(64 * z, 64), 64)
             send(src.at[rows, :], dst.at[3], pair_send.at[pair], into, k_dev, z)
 
     def settle(t):
-        _, b, _ = sides(t)
+        a, b, half = sides(t)
+        wide = 256 if t < WHOLE else 128
         if t == 0:
-            size, buf, sem = 64, parts0, part0_recv
+            buf, sem = parts0, part0_recv
         elif t < WHOLE:
-            size, buf, sem = 64, parts.at[t - 1], part_recv.at[t - 1]
+            buf, sem = parts.at[t - 1], part_recv.at[t - 1]
         else:
-            size, buf, sem = 32, half_parts.at[t - WHOLE], part_recv.at[t - 1]
+            buf, sem = half_parts.at[t - WHOLE], part_recv.at[t - 1]
         arrived(buf, sem, f"wp{t}")
         part = [buf[n].astype(F32) for n in range(7)]
-        rows = pl.ds(pl.multiple_of(size * z, size), size)
-        k = gram[t, rows, :] + ((part[0] + part[1]) + part[2])
+        rows = pl.ds(pl.multiple_of(64 * z, 64), 64)
+        k = gram[t, rows, 0:wide] + ((part[0] + part[1]) + part[2])
         l = (part[3] + part[4]) + (part[5] + part[6])
         h = k * l
-        lane = lax.broadcasted_iota(jnp.int32, (size, 128), 1)
-        own = jnp.where(lane == t, jnp.sum(h, axis=1, keepdims=True), 0.0)
+        lane = lax.broadcasted_iota(jnp.int32, (64, 128), 1)
+        row_cols[...] += jnp.where(lane == t, jnp.sum(h, axis=1, keepdims=True), 0.0)
         weight = 1.0
         if t:
             weight = 2.0
             across = jnp.sum(h, axis=0, keepdims=True)
-            col_acc[...] += jnp.where(slot_row == b, across, 0.0)
-        if t < WHOLE:
-            row_cols[...] += own
-        else:
-            half_cols[...] += own
-        acc[0, 0:size] += weight * (k * k)
-        acc[1, 0:size] += weight * (l * l)
-        acc[2, 0:size] += weight * h
+            to = b
+            if t >= WHOLE:
+                side = lax.broadcasted_iota(jnp.int32, (1, 256), 1) // 128
+                across = jnp.where(side == half, jnp.concatenate([across] * 2, axis=1), 0.0)
+                to = a
+            col_acc[...] += jnp.where(slot_row == to, across, 0.0)
+        acc[0, :, 0:wide] += weight * (k * k)
+        acc[1, :, 0:wide] += weight * (l * l)
+        acc[2, :, 0:wide] += weight * h
 
     slot_row = lax.broadcasted_iota(jnp.int32, (8, 256), 0)
 
@@ -350,7 +351,6 @@
     def _():
         acc[...] = jnp.zeros_like(acc)
         row_cols[...] = jnp.zeros_like(row_cols)
-        half_cols[...] = jnp.zeros_like(half_cols)
         col_acc[...] = jnp.zeros_like(col_acc)
         product(0)
         for j in range(PIECES):
@@ -453,23 +453,16 @@
 
     @pl.when(is_k)
     def _():
-        for t in (0, 4, 6, 5, 7, 1, 8, 2, 3):
+        for t in (0, 4, 6, 5, 7, 1, 8, 2, 3, 10, 9, 11, 12):
             settle(t)
         turned = jnp.concatenate([row_cols[...]] * 2, axis=0).T
         turned = jnp.concatenate([turned] * 2, axis=1)
-        for t in (10, 9, 11, 12):
-            settle(t)
-        half_turned = jnp.concatenate([half_cols[...]] * 4, axis=0).T
-        half_turned = jnp.concatenate([half_turned] * 2, axis=1)
-        col = lax.broadcasted_iota(jnp.int32, (1, 256), 1)
+        mine = lax.broadcasted_iota(jnp.int32, (1, 256), 1) // 64 == z
         both = col_acc[...]
         for t in range(len(TILES)):
-            a, _, half = sides(t)
-            if t < WHOLE:
-                row = jnp.where(col // 64 == z, turned[t : t + 1, :], 0.0)
-            else:
-                row = jnp.where(col // 32 == 4 * half + z, half_turned[t : t + 1, :], 0.0)
-            both = both + jnp.where(slot_row == a, row, 0.0)
+            a, b, _ = sides(t)
+            row = jnp.where(mine, turned[t : t + 1, :], 0.0)
+            both = both + jnp.where(slot_row == (a if t < WHOLE else b), row, 0.0)
         scal_lane = lax.broadcasted_iota(jnp.int32, (1, 128), 1)
         scal = jnp.zeros((1, 128), F32)
         for j in range(3):
@@ -584,8 +577,8 @@
             vm((13, 256, 256), F32),
             vm((3, 256, 256), BF16),
             vm((3, 7, 64, 256), BF16),
-            vm((9, 128, 256), BF16),
-            vm((9, 7, 32, 256), BF16),
+            vm((9, 256, 128), BF16),
+            vm((9, 7, 64, 128), BF16),
             vm((7, 64, 256), F32),
             vm((1, 2048), F32),
             vm((16, 1, 2048), F32),
@@ -596,7 +589,6 @@
             vm((32, 8192), BF16),
             vm((3, 64, 256), F32),
             vm((64, 128), F32),
-            vm((32, 128), F32),
             vm((8, 256), F32),
             vm((16, 1, 384), F32),
             vm((64, 1, 384), F32),

time: 65.6 us -> 65.6 us (level)
  no operation moved by 1% of the time
where the time goes in v12:
time: 65.6 us; the launch traced here: 65.4 us
  Pallas kernels  64.8 us (99%)
    pallas_call x1, Pallas kernels, body(): pl.pallas_call(kernel, out_shape=(jax.ShapeDtypeStruct((1, 32), F32), jax...  62.1 us
    pallas_call x1, Pallas kernels, body(): pl.pallas_call(publish, out_shape=(jax.ShapeDtypeStruct((1, 32), F32), ja...  2.71 us

profile of v12, /device:TPU:1, one launch (start us, length us, event | category | flops | bytes accessed | tf_op | source)
XLA Modules:
  0.0 65.4 jit_solution(5531837033236537274)
XLA Ops:
  0.6 62.1 %shard_map.57 = (f32[1,32]{1,0:T(1,128)}, f32[1,1]{1,0:T(1,128)}, bf16[32,8192]{1,0:T(8,128)(2,1)}, bf16[32,8192]{1,0:T(8,128)(2,1)}) custom-call(bf16[64,4096]{1,0:T(8,128)(2,1)} %bitcast.3, bf16[32,8192]{1,0:T(8,128)(2,1)} %late_hbm.1), custom_call_target="tpu_custom_call" | custom-call | tf_op jit(solution)/shard_map/pallas_call | solution.py:561
  62.7 2.7 %shard_map.58 = (f32[1,32]{1,0:T(1,128)}, f32[1,1]{1,0:T(1,128)}, bf16[32,8192]{1,0:T(8,128)(2,1)}, bf16[32,8192]{1,0:T(8,128)(2,1)}) custom-call(f32[1,32]{1,0:T(1,128)} %get-tuple-element.12.share_in, f32[1,1]{1,0:T(1,128)} %get-tuple-element.13.sim_in, bf16[32,8192]{1,0:T(8,128)(2,1)} %get-tuple-element.14.early_in, ...), custom_call_target="tpu_custom_call" | custom-call | tf_op jit(solution)/shard_map/pallas_call | solution.py:620

commit v13 on v11

--- a/solution.py
+++ b/solution.py
@@ -384,19 +384,19 @@
             from_1(near)
             from_2(far)
         late_mean()
-        center(1, 0)
-        product(4)
-        center(2, 0)
-        product(6)
+        take(3, DETOUR[0])
+        forward(3, 1, DETOUR[0], 0, 3)
+        take(3, DETOUR[1])
+        forward(3, 2, DETOUR[1], 3, 0)
         for j in (0, 1, 2, 3, 4, 7):
             if j % 2:
                 forward(1, 3, j, 0, 1)
             else:
                 forward(2, 3, j, 1, 0)
-        take(3, DETOUR[0])
-        forward(3, 1, DETOUR[0], 0, 3)
-        take(3, DETOUR[1])
-        forward(3, 2, DETOUR[1], 3, 0)
+        center(1, 0)
+        product(4)
+        center(2, 0)
+        product(6)
         from_2(DETOUR[1])
         from_1(DETOUR[0])
         center(1, 1)

time: 65.6 us -> 65.3 us (level)
  no operation moved by 1% of the time
where the time goes in v13:
time: 65.3 us; the launch traced here: 65.2 us
  Pallas kernels  64.5 us (99%)
    pallas_call x1, Pallas kernels, body(): pl.pallas_call(kernel, out_shape=(jax.ShapeDtypeStruct((1, 32), F32), jax...  61.8 us
    pallas_call x1, Pallas kernels, body(): pl.pallas_call(publish, out_shape=(jax.ShapeDtypeStruct((1, 32), F32), ja...  2.71 us

profile of v13, /device:TPU:1, one launch (start us, length us, event | category | flops | bytes accessed | tf_op | source)
XLA Modules:
  0.0 65.2 jit_solution(7958104667432364489)
XLA Ops:
  0.6 61.8 %shard_map.57 = (f32[1,32]{1,0:T(1,128)}, f32[1,1]{1,0:T(1,128)}, bf16[32,8192]{1,0:T(8,128)(2,1)}, bf16[32,8192]{1,0:T(8,128)(2,1)}) custom-call(bf16[64,4096]{1,0:T(8,128)(2,1)} %bitcast.3, bf16[32,8192]{1,0:T(8,128)(2,1)} %late_hbm.1), custom_call_target="tpu_custom_call" | custom-call | tf_op jit(solution)/shard_map/pallas_call | solution.py:568
  62.5 2.7 %shard_map.58 = (f32[1,32]{1,0:T(1,128)}, f32[1,1]{1,0:T(1,128)}, bf16[32,8192]{1,0:T(8,128)(2,1)}, bf16[32,8192]{1,0:T(8,128)(2,1)}) custom-call(f32[1,32]{1,0:T(1,128)} %get-tuple-element.12.share_in, f32[1,1]{1,0:T(1,128)} %get-tuple-element.13.sim_in, bf16[32,8192]{1,0:T(8,128)(2,1)} %get-tuple-element.14.early_in, ...), custom_call_target="tpu_custom_call" | custom-call | tf_op jit(solution)/shard_map/pallas_call | solution.py:628

commit v14 on v13

--- a/solution.py
+++ b/solution.py
@@ -388,15 +388,15 @@
         forward(3, 1, DETOUR[0], 0, 3)
         take(3, DETOUR[1])
         forward(3, 2, DETOUR[1], 3, 0)
+        center(1, 0)
+        product(4)
+        center(2, 0)
+        product(6)
         for j in (0, 1, 2, 3, 4, 7):
             if j % 2:
                 forward(1, 3, j, 0, 1)
             else:
                 forward(2, 3, j, 1, 0)
-        center(1, 0)
-        product(4)
-        center(2, 0)
-        product(6)
         from_2(DETOUR[1])
         from_1(DETOUR[0])
         center(1, 1)

time: 65.3 us -> 66.5 us (1.018)
  Pallas kernels: 64.5 us -> 65.7 us
    pallas_call x1, Pallas kernels: 61.8 us -> 63 us  [body(): pl.pallas_call(kernel, out_shape=(jax.ShapeDtypeStruct((1, 32), F32), jax...]
where the time goes in v14:
time: 66.5 us; the launch traced here: 66.4 us
  Pallas kernels  65.7 us (99%)
    pallas_call x1, Pallas kernels, body(): pl.pallas_call(kernel, out_shape=(jax.ShapeDtypeStruct((1, 32), F32), jax...  63 us
    pallas_call x1, Pallas kernels, body(): pl.pallas_call(publish, out_shape=(jax.ShapeDtypeStruct((1, 32), F32), ja...  2.71 us

profile of v14, /device:TPU:1, one launch (start us, length us, event | category | flops | bytes accessed | tf_op | source)
XLA Modules:
  0.0 66.4 jit_solution(1206880991376447495)
XLA Ops:
  0.6 63.0 %shard_map.57 = (f32[1,32]{1,0:T(1,128)}, f32[1,1]{1,0:T(1,128)}, bf16[32,8192]{1,0:T(8,128)(2,1)}, bf16[32,8192]{1,0:T(8,128)(2,1)}) custom-call(bf16[64,4096]{1,0:T(8,128)(2,1)} %bitcast.3, bf16[32,8192]{1,0:T(8,128)(2,1)} %late_hbm.1), custom_call_target="tpu_custom_call" | custom-call | tf_op jit(solution)/shard_map/pallas_call | solution.py:568
  63.6 2.7 %shard_map.58 = (f32[1,32]{1,0:T(1,128)}, f32[1,1]{1,0:T(1,128)}, bf16[32,8192]{1,0:T(8,128)(2,1)}, bf16[32,8192]{1,0:T(8,128)(2,1)}) custom-call(f32[1,32]{1,0:T(1,128)} %get-tuple-element.12.share_in, f32[1,1]{1,0:T(1,128)} %get-tuple-element.13.sim_in, bf16[32,8192]{1,0:T(8,128)(2,1)} %get-tuple-element.14.early_in, ...), custom_call_target="tpu_custom_call" | custom-call | tf_op jit(solution)/shard_map/pallas_call | solution.py:628
